TPU v7x, 32 devices: a whole 2x2x4 slice. The times are simulated.
32 devices in a mesh: fsdp: 2 (over x), heads: 4 (over y, core), tensor: 4 (over z).
Axes of the slice: x: 2, y: 2, z: 4, core: 2. Of those that a mesh axis runs over, the one named last changes fastest.
Arguments:
- inputs: bfloat16 [16, 1024, 1024], P(('fsdp', 'tensor'), 'heads')
- slot_flag: int32 [16], P(('fsdp', 'tensor')), may hold values from 0 to 1, as said below
- cotangent: bfloat16 [16, 1024, 1024], P(('fsdp', 'tensor'), 'heads'), may hold values from -6 to 6
- first_gain: bfloat16 [1024], P(('fsdp', 'heads', 'tensor')), may hold values from 0.5 to 1.5
- first_shift: bfloat16 [1024], P(('fsdp', 'heads', 'tensor')), may hold values from -1.25 to 1.25
- query_weight: bfloat16 [1024, 1024], P(('fsdp', 'heads', 'tensor')), may hold values from -0.25 to 0.25
- query_bias: bfloat16 [1024], P(('fsdp', 'heads', 'tensor')), may hold values from -1.75 to 1.75
- key_weight: bfloat16 [1024, 1024], P(('fsdp', 'heads', 'tensor')), may hold values from -0.1875 to 0.1875
- value_weight: bfloat16 [1024, 1024], P(('fsdp', 'heads', 'tensor')), may hold values from -0.1875 to 0.1875
- value_bias: bfloat16 [1024], P(('fsdp', 'heads', 'tensor')), may hold values from -0.3125 to 0.3125
- out_weight: bfloat16 [1024, 1024], P(('fsdp', 'heads', 'tensor')), may hold values from -1.5 to 1.5
- out_bias: bfloat16 [1024], P(('fsdp', 'heads', 'tensor')), may hold values from -0.625 to 0.625
- second_gain: bfloat16 [1024], P(('fsdp', 'heads', 'tensor')), may hold values from 0.5 to 1.5
- second_shift: bfloat16 [1024], P(('fsdp', 'heads', 'tensor')), may hold values from -1.25 to 1.25
- gate_weight: bfloat16 [1024, 2736], P(('fsdp', 'heads'), 'tensor'), may hold values from -0.1875 to 0.1875
- gate_bias: bfloat16 [2736], P('tensor'), may hold values from -1.75 to 1.75
- up_weight: bfloat16 [1024, 2736], P(('fsdp', 'heads'), 'tensor'), may hold values from -0.1875 to 0.1875
- up_bias: bfloat16 [2736], P('tensor'), may hold values from -1.75 to 1.75
- inner_gain: bfloat16 [2736], P('tensor'), may hold values from 0.5 to 1.5
- inner_shift: bfloat16 [2736], P('tensor'), may hold values from -1.25 to 1.25
- down_weight: bfloat16 [2736, 1024], P('tensor', ('fsdp', 'heads')), may hold values from -0.109375 to 0.109375
- down_bias: bfloat16 [1024], P(('fsdp', 'heads', 'tensor')), may hold values from -0.625 to 0.625
Outputs:
- output: bfloat16 [16, 1024, 1024], P(('fsdp', 'tensor'), 'heads')
- input_grad: bfloat16 [16, 1024, 1024], P(('fsdp', 'tensor'), 'heads')
- first_gain_grad: float32 [1024], P(('fsdp', 'heads', 'tensor'))
- first_shift_grad: float32 [1024], P(('fsdp', 'heads', 'tensor'))
- query_weight_grad: float32 [1024, 1024], P(('fsdp', 'heads', 'tensor'))
- query_bias_grad: float32 [1024], P(('fsdp', 'heads', 'tensor'))
- key_weight_grad: float32 [1024, 1024], P(('fsdp', 'heads', 'tensor'))
- value_weight_grad: float32 [1024, 1024], P(('fsdp', 'heads', 'tensor'))
- value_bias_grad: float32 [1024], P(('fsdp', 'heads', 'tensor'))
- out_weight_grad: float32 [1024, 1024], P(('fsdp', 'heads', 'tensor'))
- out_bias_grad: float32 [1024], P(('fsdp', 'heads', 'tensor'))
- second_gain_grad: float32 [1024], P(('fsdp', 'heads', 'tensor'))
- second_shift_grad: float32 [1024], P(('fsdp', 'heads', 'tensor'))
- gate_weight_grad: float32 [1024, 2736], P(('fsdp', 'heads'), 'tensor')
- gate_bias_grad: float32 [2736], P('tensor')
- up_weight_grad: float32 [1024, 2736], P(('fsdp', 'heads'), 'tensor')
- up_bias_grad: float32 [2736], P('tensor')
- inner_gain_grad: float32 [2736], P('tensor')
- inner_shift_grad: float32 [2736], P('tensor')
- down_weight_grad: float32 [2736, 1024], P('tensor', ('fsdp', 'heads'))
- down_bias_grad: float32 [1024], P(('fsdp', 'heads', 'tensor'))
Inputs may be any that keep to these rules, and one draw needn't show every extreme that they name: `slot_flag`: exactly one of the 16 image slots has flag 0; all others have flag 1.
All inputs are finite; a program needn't handle non-finite values.
Results may differ from a plain program's by a relative error of at most 0.017.
Values may be sent and summed in bfloat16 or wider, within the bound.
A program may use at most 192 MiB of HBM per device.

v0:
```python
import math

import jax
import jax.numpy as jnp
from jax import lax
from jax.experimental import pallas as pl
from jax.experimental.pallas import tpu as pltpu
from jax.sharding import PartitionSpec as P


HD = 64
PAIR = 2 * HD
FF_REAL = 2730
GRID = 32


norm_eps = 1e-06


def layer_norm(values, gain_vec, shift_vec):
    row_mean = jnp.mean(values, axis=-1, keepdims=True)
    centered = values - row_mean
    row_var = jnp.mean(centered * centered, axis=-1, keepdims=True)
    inv_std = lax.rsqrt(row_var + norm_eps)
    unit_rows = centered * inv_std
    return (unit_rows * gain_vec + shift_vec, unit_rows, inv_std)


def norm_backward(grad_values, unit_rows, inv_std, gain_vec):
    scaled = grad_values * gain_vec
    centered = scaled - jnp.mean(scaled, axis=-1, keepdims=True)
    centered = centered - unit_rows * jnp.mean(scaled * unit_rows, axis=-1, keepdims=True)
    return centered * inv_std


def rope_tables():
    positions = jnp.arange(GRID * GRID, dtype=jnp.int32)
    row_place = (positions // GRID).astype(jnp.float32)
    col_place = (positions % GRID).astype(jnp.float32)
    quarter = HD // 4
    frequency = jnp.power(10000.0, -jnp.arange(quarter, dtype=jnp.float32) / quarter)
    angles = jnp.concatenate(
        [row_place[:, None] * frequency[None, :], col_place[:, None] * frequency[None, :]], axis=1
    )
    angles = jnp.repeat(angles, 2, axis=1)
    return (jnp.cos(angles), jnp.sin(angles))


def pair_swap(values):
    count = values.shape[-1]
    lanes = lax.broadcasted_iota(jnp.int32, values.shape, 1)
    following = pltpu.roll(values, count - 1, 1)
    preceding = pltpu.roll(values, 1, 1)
    return jnp.where(lanes % 2 == 0, -following, preceding)


def rotate(values, cosine_table, sine_table):
    return values * cosine_table + pair_swap(values) * sine_table


def rotate_back(grad_values, cosine_table, sine_table):
    return grad_values * cosine_table - pair_swap(grad_values * sine_table)


def outer_product(left_rows, right_rows):
    return lax.dot_general(
        left_rows, right_rows, (((0,), (0,)), ((), ())), preferred_element_type=jnp.float32
    )


def times_transpose(left_rows, right_rows):
    return lax.dot_general(
        left_rows, right_rows, (((1,), (1,)), ((), ())), preferred_element_type=jnp.float32
    )


def gather_rows(block_values):
    return lax.all_gather(block_values, "tensor", axis=0, tiled=True)


def tensor_sums(first_sum, second_sum):
    both = lax.psum(jnp.stack([first_sum, second_sum]).astype(jnp.bfloat16), "tensor")
    return (both[0].astype(jnp.float32), both[1].astype(jnp.float32))


def cube_pairs(ways, bit):
    return [(place, place ^ (1 << bit)) for place in range(ways)]


def cube_gather(block, axis_name):
    ways = lax.axis_size(axis_name)
    bits = ways.bit_length() - 1
    index = lax.axis_index(axis_name)
    held = block.reshape((1,) * bits + block.shape)
    for bit in reversed(range(bits)):
        place = bits - 1 - bit
        other = lax.ppermute(held, axis_name, cube_pairs(ways, bit))
        held = jnp.where(
            (index >> bit) % 2 == 0,
            jnp.concatenate([held, other], axis=place),
            jnp.concatenate([other, held], axis=place),
        )
    return held.reshape((ways * block.shape[0],) + block.shape[1:])


def cube_scatter(terms, axis_name):
    ways = lax.axis_size(axis_name)
    bits = ways.bit_length() - 1
    index = lax.axis_index(axis_name)
    held = terms.reshape((2,) * bits + terms.shape[1:])
    for bit in range(bits):
        place = bits - 1 - bit
        mine = (index >> bit) % 2
        kept = lax.dynamic_index_in_dim(held, mine, place, keepdims=False)
        sent = lax.dynamic_index_in_dim(held, 1 - mine, place, keepdims=False)
        other = lax.ppermute(sent.astype(jnp.bfloat16), axis_name, cube_pairs(ways, bit))
        held = kept.astype(jnp.float32) + other.astype(jnp.float32)
    return held


def line_pairs(ways):
    upward = [(place, place + 1) for place in range(ways - 1)]
    return (upward, [(target, source) for source, target in upward])


def line_step(below, above, axis_name):
    upward, downward = line_pairs(lax.axis_size(axis_name))
    below.append(lax.ppermute(below[-1], axis_name, upward))
    above.append(lax.ppermute(above[-1], axis_name, downward))


def line_pick(below, above, axis_name):
    ways = lax.axis_size(axis_name)
    block = below[0]
    around = jnp.stack(below[:0:-1] + [block] + above[1:])
    picked = lax.dynamic_slice_in_dim(around, ways - 1 - lax.axis_index(axis_name), ways, 0)
    return picked.reshape((ways * block.shape[0],) + block.shape[1:])


def after(value, *others):
    return lax.optimization_barrier((value,) + others)[0]


def line_term(terms, offset, axis_name):
    place = lax.axis_index(axis_name) + offset
    place = jnp.clip(place, 0, lax.axis_size(axis_name) - 1)
    return lax.dynamic_index_in_dim(terms, place, 0, keepdims=False).astype(jnp.float32)


def line_scatter_step(terms, running, distance, axis_name, gate):
    pairs = line_pairs(lax.axis_size(axis_name))
    passed = []
    for side, sign in ((0, 1), (1, -1)):
        total = line_term(terms, sign * distance, axis_name)
        if running is not None:
            total = total + running[side].astype(jnp.float32)
        gated = after(total.astype(jnp.bfloat16), gate)
        passed.append(lax.ppermute(gated, axis_name, pairs[side]))
    return passed


def scatter_rows(term_fn, row_total):
    return lax.psum_scatter(
        term_fn(jnp.int32(0), row_total * lax.axis_size("tensor")).astype(jnp.bfloat16),
        "tensor",
        scatter_dimension=0,
        tiled=True,
    ).astype(jnp.float32)


def head_masks(axis):
    shape = (1, PAIR) if axis == 1 else (PAIR, 1)
    place = lax.broadcasted_iota(jnp.int32, shape, axis)
    first = (place < HD).astype(jnp.float32)
    return (first, 1.0 - first)


def load_heads(qkv_ref, cosine_ref, sine_ref, query_s, key_s, value_s):
    rows = qkv_ref[...].reshape(query_s.shape[0], 3 * PAIR)
    cosine, sine = cosine_ref[...], sine_ref[...]
    query_rot = rotate(rows[:, :PAIR].astype(jnp.float32), cosine, sine).astype(jnp.bfloat16)
    query_s[...] = (query_rot.astype(jnp.float32) * (1.0 / math.sqrt(HD))).astype(jnp.bfloat16)
    key_rot = rotate(rows[:, PAIR : 2 * PAIR].astype(jnp.float32), cosine, sine)
    key_s[...] = key_rot.astype(jnp.bfloat16)
    value_s[...] = rows[:, 2 * PAIR :]


def forward_kernel(qkv_ref, cosine_ref, sine_ref, mixed_ref, query_s, key_s, value_s):
    load_heads(qkv_ref, cosine_ref, sine_ref, query_s, key_s, value_s)
    pieces, _, piece_len, _ = mixed_ref.shape
    masks = head_masks(1)

    def one_piece(piece, carry):
        start = pl.multiple_of(piece * piece_len, piece_len)
        query_rows = query_s[pl.ds(start, piece_len), :]
        mixed = jnp.zeros((piece_len, PAIR), jnp.float32)
        for mask in masks:
            own_query = query_rows * mask.astype(jnp.bfloat16)
            scores = times_transpose(own_query, key_s[...])
            weights_exp = jnp.exp(scores - jnp.max(scores, axis=-1, keepdims=True))
            inverse = 1.0 / jnp.sum(weights_exp, axis=-1, keepdims=True)
            probs_low = (weights_exp * inverse).astype(jnp.bfloat16)
            part = jnp.dot(probs_low, value_s[...], preferred_element_type=jnp.float32)
            mixed = mixed + part * mask
        mixed_ref[piece, 0] = mixed.astype(jnp.bfloat16)
        return carry

    lax.fori_loop(0, pieces, one_piece, 0)


def backward_kernel(
    qkv_ref, grad_ref, cosine_ref, sine_ref, out_ref,
    query_s, key_s, value_s, turned_s, key_grad_s, value_grad_s,
):
    load_heads(qkv_ref, cosine_ref, sine_ref, query_s, key_s, value_s)
    pieces, _, piece_len, _ = grad_ref.shape
    turned_s[...] = key_s[...].astype(jnp.float32).T.astype(jnp.bfloat16)
    key_grad_s[...] = jnp.zeros_like(key_grad_s)
    value_grad_s[...] = jnp.zeros_like(value_grad_s)
    row_masks = head_masks(1)
    column_masks = head_masks(0)

    def one_piece(piece, carry):
        start = pl.multiple_of(piece * piece_len, piece_len)
        rows = pl.ds(start, piece_len)
        query_rows = query_s[rows, :]
        grad_rows = grad_ref[piece, 0]
        query_grad = jnp.zeros((PAIR, piece_len), jnp.float32)
        for mask, column_mask in zip(row_masks, column_masks):
            own_query = query_rows * mask.astype(jnp.bfloat16)
            own_grad = grad_rows * mask.astype(jnp.bfloat16)
            scores = times_transpose(key_s[...], own_query)
            weights_exp = jnp.exp(scores - jnp.max(scores, axis=0, keepdims=True))
            probs = weights_exp * (1.0 / jnp.sum(weights_exp, axis=0, keepdims=True))
            grad_probs = times_transpose(value_s[...], own_grad)
            row_dot = jnp.sum(grad_probs * probs, axis=0, keepdims=True)
            grad_scores = (probs * (grad_probs - row_dot)).astype(jnp.bfloat16)
            value_grad_s[...] += jnp.dot(
                probs.astype(jnp.bfloat16), own_grad, preferred_element_type=jnp.float32
            )
            key_grad_s[...] += jnp.dot(grad_scores, own_query, preferred_element_type=jnp.float32)
            own_turned = turned_s[...] * column_mask.astype(jnp.bfloat16)
            query_grad = query_grad + jnp.dot(
                own_turned, grad_scores, preferred_element_type=jnp.float32
            )
        query_grad = query_grad.T * (1.0 / math.sqrt(HD))
        turned = rotate_back(query_grad, cosine_ref[rows, :], sine_ref[rows, :])
        out_ref[piece, 0, :, :PAIR] = turned.astype(jnp.bfloat16)
        return carry

    lax.fori_loop(0, pieces, one_piece, 0)
    piece_shape = (pieces, 1, piece_len, PAIR)
    key_grad = rotate_back(key_grad_s[...], cosine_ref[...], sine_ref[...])
    out_ref[:, :, :, PAIR : 2 * PAIR] = key_grad.astype(jnp.bfloat16).reshape(piece_shape)
    out_ref[:, :, :, 2 * PAIR :] = value_grad_s[...].astype(jnp.bfloat16).reshape(piece_shape)


def attention_call(kernel, qkv, extra, tables, out_lanes, more_scratch, products):
    pieces, seq_count, piece_len, lanes = qkv.shape
    pair_count = lanes // (3 * PAIR)
    length = pieces * piece_len

    def per_pair(wide):
        return pl.BlockSpec((pieces, 1, piece_len, wide), lambda seq, pair: (0, seq, 0, pair))

    table_spec = pl.BlockSpec((length, PAIR), lambda seq, pair: (0, 0))
    blocks = seq_count * pair_count
    return pl.pallas_call(
        kernel,
        grid=(seq_count, pair_count),
        in_specs=[per_pair(3 * PAIR)] + [per_pair(PAIR)] * len(extra) + [table_spec] * 2,
        out_specs=per_pair(out_lanes),
        out_shape=jax.ShapeDtypeStruct(
            (pieces, seq_count, piece_len, pair_count * out_lanes), jnp.bfloat16
        ),
        scratch_shapes=[pltpu.VMEM((length, PAIR), jnp.bfloat16)] * 3 + more_scratch,
        compiler_params=pltpu.CompilerParams(vmem_limit_bytes=48 << 20),
        cost_estimate=pl.CostEstimate(
            flops=blocks * products * 4 * length * length * PAIR,
            bytes_accessed=blocks * length * PAIR * 16,
            transcendentals=blocks * 2 * length * length,
        ),
    )(qkv, *extra, *tables)


def attend_forward(qkv, tables):
    return attention_call(forward_kernel, qkv, (), tables, PAIR, [], 2)


def attend_backward(qkv, grad_mixed, tables):
    length = qkv.shape[0] * qkv.shape[2]
    more = [
        pltpu.VMEM((PAIR, length), jnp.bfloat16),
        pltpu.VMEM((length, PAIR), jnp.float32),
        pltpu.VMEM((length, PAIR), jnp.float32),
    ]
    return attention_call(backward_kernel, qkv, (grad_mixed,), tables, 3 * PAIR, more, 5)


def hidden_forward(token_rows, gate_part, up_part, gate_shift, up_shift, unit_mask):
    gate_pre = jnp.dot(token_rows, gate_part, preferred_element_type=jnp.float32) + gate_shift
    up_pre = jnp.dot(token_rows, up_part, preferred_element_type=jnp.float32) + up_shift
    return (gate_pre, up_pre, jax.nn.silu(gate_pre) * up_pre * unit_mask)


def inner_normalize(hidden, first_sum, second_sum, inner_scale, inner_offset, unit_mask):
    unit_mean = first_sum[:, None] / FF_REAL
    unit_var = second_sum[:, None] / FF_REAL - unit_mean * unit_mean
    inv_std = lax.rsqrt(unit_var + norm_eps)
    unit_hidden = (hidden - unit_mean) * inv_std
    normed = ((unit_hidden * inner_scale + inner_offset) * unit_mask).astype(jnp.bfloat16)
    return (normed, unit_hidden, inv_std)


def hidden_backward_terms(grad_normed, unit_hidden, inner_scale, unit_mask):
    scaled = grad_normed * unit_mask * inner_scale
    return (scaled, jnp.sum(scaled, axis=-1), jnp.sum(scaled * unit_hidden, axis=-1))


def gate_grads(scaled, scaled_sum, cross_sum, unit_hidden, inv_std, gate_pre, up_pre, unit_mask):
    grad_hidden = (
        unit_mask
        * (scaled - scaled_sum[:, None] / FF_REAL - unit_hidden * cross_sum[:, None] / FF_REAL)
        * inv_std
    )
    sigmoid_gate = jax.nn.sigmoid(gate_pre)
    grad_gate = (
        grad_hidden * up_pre * sigmoid_gate * (1.0 + gate_pre * (1.0 - sigmoid_gate))
    ).astype(jnp.bfloat16)
    grad_up = (grad_hidden * gate_pre * sigmoid_gate).astype(jnp.bfloat16)
    return (grad_gate, grad_up)


def vector_sums(grad_gate, grad_up, grad_normed, unit_hidden, unit_mask):
    return (
        jnp.sum(grad_gate, axis=0, dtype=jnp.float32),
        jnp.sum(grad_up, axis=0, dtype=jnp.float32),
        jnp.sum(grad_normed * unit_mask * unit_hidden, axis=0),
        jnp.sum(grad_normed * unit_mask, axis=0),
    )


def on_device(
    inputs,
    slot_flag,
    cotangent,
    first_gain,
    first_shift,
    query_weight,
    query_bias,
    key_weight,
    value_weight,
    value_bias,
    out_weight,
    out_bias,
    second_gain,
    second_shift,
    gate_weight,
    gate_bias,
    up_weight,
    up_bias,
    inner_gain,
    inner_shift,
    down_weight,
    down_bias,
):
    seq_local, piece_len, width = inputs.shape
    head_ways = lax.axis_size("heads")
    group_width = width // head_ways
    group_pairs = group_width // PAIR
    token_count = seq_local * piece_len
    fsdp_ways, tensor_ways = lax.axis_size("fsdp"), lax.axis_size("tensor")
    row_part = query_weight.shape[0]
    group_index = lax.axis_index("heads")
    inputs_group = cube_gather(inputs, "heads")
    grad_flags = slot_flag.astype(jnp.float32)[:, None, None]
    grad_total = grad_flags * cotangent.astype(jnp.float32)
    grad_branch = grad_total.astype(jnp.bfloat16)
    below, above = [grad_branch], [grad_branch]
    line_step(below, above, "tensor")
    below[-1], above[-1] = after(below[-1], inputs_group), after(above[-1], inputs_group)
    line_step(below, above, "tensor")
    stacked = jnp.stack(
        [
            member.reshape(row_part, head_ways, group_pairs, PAIR)
            for member in (query_weight, key_weight, value_weight)
        ],
        axis=3,
    ).reshape(row_part, head_ways, 3 * group_width)
    vectors = (
        first_gain,
        first_shift,
        query_bias,
        value_bias,
        out_bias,
        second_gain,
        second_shift,
        down_bias,
    )
    row_lanes = 3 * group_width
    vector_row = jnp.zeros((row_lanes,), jnp.float32)
    for place, member in enumerate(vectors):
        ahead = place * row_part
        vector_row = vector_row + jnp.pad(
            member.astype(jnp.float32), (ahead, row_lanes - ahead - row_part)
        )
    vector_row = vector_row.astype(jnp.bfloat16)
    sent_columns = jnp.concatenate(
        [
            stacked.transpose(1, 0, 2),
            jnp.broadcast_to(vector_row, (head_ways, 1, 3 * group_width)),
        ],
        axis=1,
    )
    own_columns = lax.all_to_all(
        sent_columns, "heads", split_axis=0, concat_axis=0, tiled=True
    )
    columns = lax.all_gather(
        own_columns.reshape(-1, 3 * group_width), ("fsdp", "tensor"), axis=0, tiled=True
    )
    group_f = inputs_group.reshape(-1, width).astype(jnp.float32)
    group_mean = jnp.mean(group_f, axis=-1, keepdims=True)
    group_var = jnp.mean(jnp.square(group_f - group_mean), axis=-1, keepdims=True)
    group_inv = lax.rsqrt(group_var + norm_eps)
    columns, group_mean, group_inv = lax.optimization_barrier((columns, group_mean, group_inv))
    columns = columns.reshape(
        fsdp_ways, tensor_ways, head_ways, row_part + 1, 3 * group_width
    ).transpose(0, 2, 1, 3, 4)
    qkv_part = columns[:, :, :, :row_part].reshape(width, 3 * group_width)
    below[-1], above[-1] = after(below[-1], columns), after(above[-1], columns)
    line_step(below, above, "tensor")
    gathered = (
        columns[:, :, :, row_part, : len(vectors) * row_part]
        .reshape(-1, 8, row_part)
        .transpose(1, 0, 2)
        .reshape(8, width)
    )
    out_below, out_above = [out_weight], [out_weight]
    for _ in range(tensor_ways - 1):
        line_step(out_below, out_above, "tensor")
    out_full = lax.all_gather(
        line_pick(out_below, out_above, "tensor"),
        ("fsdp", "heads"),
        axis=0,
        tiled=True,
    )
    gain_one, shift_one, query_shift, value_shift, out_shift, gain_two, shift_two, down_shift = [
        member.astype(jnp.float32) for member in gathered
    ]
    gate_part, up_part, down_part = (
        lax.all_gather(gate_weight, ("fsdp", "heads"), axis=0, tiled=True),
        lax.all_gather(up_weight, ("fsdp", "heads"), axis=0, tiled=True),
        lax.all_gather(down_weight, ("fsdp", "heads"), axis=1, tiled=True),
    )
    inputs_f = inputs.astype(jnp.float32)
    _, unit_one, inv_one = layer_norm(inputs_f, gain_one, shift_one)
    unit_group = (group_f - group_mean) * group_inv
    low_one = (unit_group * gain_one + shift_one).astype(jnp.bfloat16)

    def group_lanes(full_vec):
        own = lax.dynamic_slice_in_dim(full_vec, group_index * group_width, group_width, 0)
        return own.reshape(group_pairs, PAIR)

    query_lanes, value_lanes = group_lanes(query_shift), group_lanes(value_shift)
    qkv_shift = jnp.stack([query_lanes, jnp.zeros_like(query_lanes), value_lanes], axis=1)
    qkv_lin = (
        (jnp.dot(low_one, qkv_part, preferred_element_type=jnp.float32) + qkv_shift.reshape(-1))
        .astype(jnp.bfloat16)
        .reshape(head_ways, seq_local, piece_len, 3 * group_width)
    )
    tables = tuple(jnp.tile(table, (1, PAIR // HD)) for table in rope_tables())
    mixed_heads = attend_forward(qkv_lin, tables)
    mixed_heads, below[-1], above[-1] = lax.optimization_barrier(
        (mixed_heads, below[-1], above[-1])
    )
    for _ in range(tensor_ways - 4):
        line_step(below, above, "tensor")
    mixed_parts = lax.all_to_all(mixed_heads, "heads", split_axis=0, concat_axis=0, tiled=True)
    grad_rows = line_pick(below, above, "tensor").reshape(-1, width)
    mixed_flat = mixed_parts.transpose(1, 2, 0, 3).reshape(token_count, width)
    residual = inputs_f + (
        jnp.dot(mixed_flat, out_full, preferred_element_type=jnp.float32) + out_shift
    ).reshape(inputs.shape)
    normed_two, unit_two, inv_two = layer_norm(residual, gain_two, shift_two)
    low_two = normed_two.astype(jnp.bfloat16)
    flag_rows = slot_flag.astype(jnp.float32)[:, None, None]
    down_shift_grad = jnp.sum(grad_branch.reshape(token_count, width), axis=0, dtype=jnp.float32)
    ffn_local = gate_part.shape[1]
    token_rows3 = gather_rows(after(low_two, gate_part, up_part, below[-1], above[-1]))
    token_rows = token_rows3.reshape(-1, width)
    col_index = lax.axis_index("tensor") * ffn_local + jnp.arange(ffn_local, dtype=jnp.int32)
    unit_mask = (col_index < FF_REAL).astype(jnp.float32)
    gate_pre, up_pre, hidden = hidden_forward(
        token_rows,
        gate_part,
        up_part,
        gate_bias.astype(jnp.float32),
        up_bias.astype(jnp.float32),
        unit_mask,
    )
    first_sum, second_sum = tensor_sums(jnp.sum(hidden, axis=-1), jnp.sum(hidden * hidden, axis=-1))
    inner_scale = inner_gain.astype(jnp.float32)
    normed_hidden, unit_hidden, inv_hidden = inner_normalize(
        hidden, first_sum, second_sum, inner_scale, inner_shift.astype(jnp.float32), unit_mask
    )
    hidden_seqs = normed_hidden.reshape(token_rows3.shape[0], piece_len, ffn_local)

    def down_term(row_count):
        picked = hidden_seqs.reshape(-1, ffn_local)
        return jnp.dot(picked, down_part, preferred_element_type=jnp.float32).reshape(
            row_count, piece_len, width
        )

    down_grad = outer_product(normed_hidden, grad_rows)
    down_weight_grad = lax.psum_scatter(
        down_grad.astype(jnp.bfloat16), ("fsdp", "heads"), scatter_dimension=1, tiled=True
    )
    grad_normed = times_transpose(after(grad_rows, down_grad), down_part)
    scaled, scaled_sum, cross_sum = hidden_backward_terms(
        grad_normed, unit_hidden, inner_scale, unit_mask
    )
    scaled_sum, cross_sum = tensor_sums(scaled_sum, cross_sum)
    grad_gate, grad_up = gate_grads(
        scaled, scaled_sum, cross_sum, unit_hidden, inv_hidden, gate_pre, up_pre, unit_mask
    )
    gate_grad = outer_product(token_rows, grad_gate)
    up_grad = outer_product(token_rows, grad_up)
    vector_grads = vector_sums(grad_gate, grad_up, grad_normed, unit_hidden, unit_mask)
    gate_seqs = after(grad_gate, down_weight_grad).reshape(-1, piece_len, ffn_local)
    up_seqs = grad_up.reshape(-1, piece_len, ffn_local)

    def input_term(row_start, row_count):
        picked_gate = gate_seqs.reshape(-1, ffn_local)
        picked_up = up_seqs.reshape(-1, ffn_local)
        summed = times_transpose(picked_gate, gate_part) + times_transpose(picked_up, up_part)
        return summed.reshape(row_count, piece_len, width)

    grad_normed_two = scatter_rows(input_term, seq_local)
    gate_weight_grad, up_weight_grad = (
        lax.psum_scatter(
            gate_grad.astype(jnp.bfloat16), ("fsdp", "heads"), scatter_dimension=0, tiled=True
        ).astype(jnp.float32),
        lax.psum_scatter(
            up_grad.astype(jnp.bfloat16), ("fsdp", "heads"), scatter_dimension=0, tiled=True
        ).astype(jnp.float32),
    )
    down_weight_grad = down_weight_grad.astype(jnp.float32)
    gate_bias_grad, up_bias_grad, inner_gain_grad, inner_shift_grad = lax.psum(
        (vector_grads[0], vector_grads[1], vector_grads[2], vector_grads[3]), ("fsdp", "heads")
    )
    grad_normed_two = after(grad_normed_two, gate_bias_grad)
    grad_residual = grad_total + norm_backward(grad_normed_two, unit_two, inv_two, gain_two)
    gain_two_grad = jnp.sum((grad_normed_two * unit_two).reshape(token_count, width), axis=0)
    shift_two_grad = jnp.sum(grad_normed_two.reshape(token_count, width), axis=0)
    grad_attn = grad_residual.astype(jnp.bfloat16).reshape(token_count, width)
    out_weight_part = outer_product(mixed_flat, grad_attn)
    out_shift_grad = jnp.sum(grad_attn, axis=0, dtype=jnp.float32)
    grad_mixed = times_transpose(grad_attn, out_full).astype(jnp.bfloat16)
    grad_parts = grad_mixed.reshape(seq_local, piece_len, head_ways, group_width)
    grad_heads = lax.all_to_all(
        grad_parts.transpose(2, 0, 1, 3), "heads", split_axis=0, concat_axis=0, tiled=True
    )
    branch_terms = down_term(seq_local * tensor_ways).astype(jnp.bfloat16)
    branch_terms = branch_terms.reshape((tensor_ways,) + inputs.shape)
    running = line_scatter_step(branch_terms, None, tensor_ways - 1, "tensor", grad_mixed)
    qkv_grad = attend_backward(qkv_lin, grad_heads, tables)
    qkv_grad = after(qkv_grad, *running)
    for distance in range(tensor_ways - 2, 0, -1):
        running = line_scatter_step(branch_terms, running, distance, "tensor", qkv_grad)
    branch_out = (
        line_term(branch_terms, 0, "tensor")
        + running[0].astype(jnp.float32)
        + running[1].astype(jnp.float32)
    )
    output = (flag_rows * (residual + branch_out + down_shift)).astype(jnp.bfloat16)
    qkv_grad = qkv_grad.reshape(head_ways * token_count, 3 * group_width)
    group_grad = times_transpose(qkv_grad, qkv_part)
    gain_one_grad = jnp.sum(group_grad * unit_group, axis=0)
    shift_one_grad = jnp.sum(group_grad, axis=0)
    group_terms = group_grad.astype(jnp.bfloat16)
    grad_normed_one = cube_scatter(
        group_terms.reshape((head_ways,) + inputs.shape), "heads"
    )
    qkv_shift_grad = jnp.sum(qkv_grad, axis=0, dtype=jnp.float32).reshape(group_pairs, 3, PAIR)

    def place_lanes(own_lanes):
        return lax.dynamic_update_slice_in_dim(
            jnp.zeros((width,), jnp.float32), own_lanes.reshape(-1), group_index * group_width, 0
        )

    query_shift_grad = place_lanes(qkv_shift_grad[:, 0])
    value_shift_grad = place_lanes(qkv_shift_grad[:, 2])
    input_grad = (
        grad_residual + norm_backward(grad_normed_one, unit_one, inv_one, gain_one)
    ).astype(jnp.bfloat16)
    vector_terms = jnp.stack(
        [
            gain_one_grad,
            shift_one_grad,
            query_shift_grad,
            value_shift_grad,
            out_shift_grad,
            gain_two_grad,
            shift_two_grad,
            down_shift_grad,
        ]
    )
    vector_lanes = vector_terms.shape[0] * row_part
    vector_rows = (
        vector_terms.reshape(-1, fsdp_ways, head_ways, tensor_ways, row_part)
        .transpose(1, 3, 2, 0, 4)
        .reshape(fsdp_ways, tensor_ways, head_ways, 1, vector_lanes)
    )
    extra_rows = 1
    while head_ways * (row_part + extra_rows) % 16 != 0:
        extra_rows += 1
    vector_rows = jnp.pad(
        vector_rows,
        ((0, 0),) * 3 + ((0, extra_rows - 1), (0, 3 * group_width - vector_lanes)),
    )
    qkv_terms = outer_product(low_one, qkv_grad).astype(jnp.bfloat16)
    qkv_terms = qkv_terms.reshape(
        fsdp_ways, head_ways, tensor_ways, row_part, 3 * group_width
    ).transpose(0, 2, 1, 3, 4)
    qkv_terms = jnp.concatenate([qkv_terms, vector_rows.astype(jnp.bfloat16)], axis=3)
    qkv_half = cube_scatter(
        qkv_terms.reshape(fsdp_ways, -1, 3 * group_width), "fsdp"
    ).astype(jnp.bfloat16)
    qkv_rows = lax.psum_scatter(qkv_half, "tensor", scatter_dimension=0, tiled=True)
    qkv_columns = lax.all_to_all(
        qkv_rows, "heads", split_axis=0, concat_axis=0, tiled=True
    ).reshape(head_ways, row_part + extra_rows, 3 * group_width)
    qkv_weight_grads = (
        qkv_columns[:, :row_part]
        .reshape(head_ways, row_part, group_pairs, 3, PAIR)
        .transpose(3, 1, 0, 2, 4)
        .reshape(3, row_part, width)
        .astype(jnp.float32)
    )
    own_sums = jnp.sum(
        qkv_columns[:, row_part, :vector_lanes].astype(jnp.float32), axis=0
    ).reshape(-1, row_part)
    out_terms = out_weight_part.astype(jnp.bfloat16).reshape(fsdp_ways, -1, width)
    out_half = cube_scatter(out_terms, "fsdp").astype(jnp.bfloat16)
    out_eighth = cube_scatter(out_half.reshape(head_ways, -1, width), "heads")
    out_weight_grad = lax.psum_scatter(
        out_eighth.astype(jnp.bfloat16), "tensor", scatter_dimension=0, tiled=True
    ).astype(jnp.float32)
    attn_sums = tuple(qkv_weight_grads) + (out_weight_grad,) + tuple(own_sums)
    return (
        output,
        input_grad,
        attn_sums[4],
        attn_sums[5],
        attn_sums[0],
        attn_sums[6],
        attn_sums[1],
        attn_sums[2],
        attn_sums[7],
        attn_sums[3],
        attn_sums[8],
        attn_sums[9],
        attn_sums[10],
        gate_weight_grad,
        gate_bias_grad,
        up_weight_grad,
        up_bias_grad,
        inner_gain_grad,
        inner_shift_grad,
        down_weight_grad,
        attn_sums[11],
    )


def solution(mesh):
    return jax.shard_map(
        on_device,
        mesh=mesh,
        in_specs=(
            P(("fsdp", "tensor"), "heads", None),
            P(("fsdp", "tensor")),
            P(("fsdp", "tensor"), "heads", None),
            P(("fsdp", "heads", "tensor")),
            P(("fsdp", "heads", "tensor")),
            P(("fsdp", "heads", "tensor"), None),
            P(("fsdp", "heads", "tensor")),
            P(("fsdp", "heads", "tensor"), None),
            P(("fsdp", "heads", "tensor"), None),
            P(("fsdp", "heads", "tensor")),
            P(("fsdp", "heads", "tensor"), None),
            P(("fsdp", "heads", "tensor")),
            P(("fsdp", "heads", "tensor")),
            P(("fsdp", "heads", "tensor")),
            P(("fsdp", "heads"), "tensor"),
            P("tensor"),
            P(("fsdp", "heads"), "tensor"),
            P("tensor"),
            P("tensor"),
            P("tensor"),
            P("tensor", ("fsdp", "heads")),
            P(("fsdp", "heads", "tensor")),
        ),
        out_specs=(
            P(("fsdp", "tensor"), "heads", None),
            P(("fsdp", "tensor"), "heads", None),
            P(("fsdp", "heads", "tensor")),
            P(("fsdp", "heads", "tensor")),
            P(("fsdp", "heads", "tensor"), None),
            P(("fsdp", "heads", "tensor")),
            P(("fsdp", "heads", "tensor"), None),
            P(("fsdp", "heads", "tensor"), None),
            P(("fsdp", "heads", "tensor")),
            P(("fsdp", "heads", "tensor"), None),
            P(("fsdp", "heads", "tensor")),
            P(("fsdp", "heads", "tensor")),
            P(("fsdp", "heads", "tensor")),
            P(("fsdp", "heads"), "tensor"),
            P("tensor"),
            P(("fsdp", "heads"), "tensor"),
            P("tensor"),
            P("tensor"),
            P("tensor"),
            P("tensor", ("fsdp", "heads")),
            P(("fsdp", "heads", "tensor")),
        ),
        check_vma=False,
    )
```

profile of v0, /device:TPU:0, one launch (start us, length us, event | category | flops | bytes accessed | tf_op | source)
XLA Modules:
  0.0 692.7 jit_solution(3502130643796988918)
XLA Ops:
  11.8 9.9 %all_to_all.24 = bf16[4,33,768]{2,1,0:T(8,128)(2,1)S(1)} all-to-all(bf16[4,33,768]{2,1,0:T(8,128)(2,1)S(1)} %pad_maximum_fusion.1), channel_id=1, replica_groups=mesh['fsdp'=2,'heads'=4,'tensor'=4] {'heads'}, dimensions={0} | all-to-all | bytes 405504 | tf_op jit(solution)/shard_map/all_to_all | solution.py:415
  27.9 4.3 collective-permute-start.9
  34.8 4.4 collective-permute-start.10
  41.8 3.9 collective-permute-done.13
  47.5 21.3 %collective-permute-done = bf16[1,1,2,256,1024]{4,3,2,1,0:T(8,128)(2,1)S(1)} collective-permute-done((bf16[1,1,2,256,1024]{4,3,2,1,0:T(8,128)(2,1)S(1)}, bf16[1,1,2,256,1024]{4,3,2,1,0:T(8,128)(2,1)S(1)}, u32[]{:S(2)}, u32[]{:S(2)}) %collective-permute-start) | collective-permute-done | bytes 1048608 | tf_op jit(solution)/shard_map/ppermute | solution.py:97
  72.2 5.5 collective-permute-start.2
  84.0 6.2 convert_reduce_fusion.1
  93.2 5.5 collective-permute-done.5
  99.8 5.5 collective-permute-start.3
  117.8 3.8 add_convert_fusion.1
  121.7 5.1 collective-permute-done.3
  126.8 4.4 collective-permute-start.4
  137.0 25.2 %shard_map.373 = bf16[4,2,256,256]{3,2,1,0:T(8,128)(2,1)} custom-call(bf16[4,2,256,768]{3,2,1,0:T(8,128)(2,1)S(1)} %bitcast.199, f32[1024,128]{1,0:T(8,128)S(1)} %copy.82.cosine_ref, f32[1024,128]{1,0:T(8,128)S(1)} %copy.83.sine_ref), custom_call_target="tpu_custom_call" | custom-call | flops 4294967296 | bytes 8388608 | tf_op jit(solution)/shard_map/pallas_call | solution.py:268
  167.8 13.3 %all-to-all-done.1 = bf16[4,2,256,256]{3,2,1,0:T(8,128)(2,1)S(1)} async-done(((bf16[4,2,256,256]{3,2,1,0:T(8,128)(2,1)}), bf16[4,2,256,256]{3,2,1,0:T(8,128)(2,1)S(1)}, u32[]{:S(2)}, u32[]{:S(2)}) %all-to-all-start.1) | async-done | bytes 1048608 | tf_op jit(solution)/shard_map/all_to_all | solution.py:478
  187.9 10.1 %all-gather.12.cloned.1.call-done = bf16[1024,684]{0,1:T(8,128)(2,1)} async-done(((bf16[128,684]{0,1:T(8,128)(2,1)}), bf16[1024,684]{0,1:T(8,128)(2,1)}) %all-gather.12.cloned.1.call-update) | async-done | bytes 1400848 | tf_op jit(solution)/shard_map/all_gather | solution.py:452
  209.3 71.5 %all-gather.14.cloned.1.call-done = bf16[8,256,1024]{2,1,0:T(8,128)(2,1)} async-done(((bf16[2,256,1024]{2,1,0:T(8,128)(2,1)}), bf16[8,256,1024]{2,1,0:T(8,128)(2,1)}) %all-gather.14.cloned.1.call-update) | async-done | bytes 4194320 | tf_op jit(solution)/shard_map/all_gather | solution.py:78
  280.8 5.5 fusion.65
  286.3 7.6 %fusion.57 = (bf16[2048]{0:T(1024)(128)(2,1)S(1)}, bf16[2048]{0:T(1024)(128)(2,1)S(1)}, f32[2048,684]{0,1:T(8,128)}, f32[2048,684]{0,1:T(8,128)}) fusion(f32[684]{0:T(1024)S(1)} %fusion.54, f32[684]{0:T(1024)S(1)} %convert_element_type.487, f32[2048,684]{0,1:T(8,128)S(1)} %fusion.65, f32[684]{0:T(1024)S(1)} %convert_element_type.486, ...), kind=kOutput, calls=%fused_computation.192 | convolution fusion | flops 2884308992 | bytes 22421520 | tf_op jit(solution)/shard_map/dot_general | solution.py:302
  294.0 9.5 %psum.42 = bf16[2,2048]{1,0:T(2,128)(2,1)S(1)} all-reduce(bf16[2,2048]{1,0:T(2,128)(2,1)S(1)} %pad_maximum_fusion.3), channel_id=1, replica_groups=mesh['fsdp'=2,'heads'=4,'tensor'=4] {'tensor'}, use_global_device_ids=true, to_apply=%region_6.7 | all-reduce | flops 4096 | bytes 16384 | tf_op jit(solution)/shard_map/psum | solution.py:82
  303.5 3.6 multiply_convert_fusion.2
  308.8 4.1 fusion.66
  315.5 10.7 %multiply_reduce_fusion.1 = (f32[684]{0:T(1024)S(1)}, bf16[2048]{0:T(1024)(128)(2,1)S(1)}, bf16[2048]{0:T(1024)(128)(2,1)S(1)}, f32[684]{0:T(1024)S(1)}, f32[2048,684]{0,1:T(8,128)}) fusion(f32[2048,684]{0,1:T(8,128)} %get-tuple-element.97, f32[2048]{0:T(1024)S(1)} %add_rsqrt_fusion, f32[2048]{0:T(1024)S(1)} %bitcast.243, f32[684]{0:T(1024)S(1)} %fusion.54, ...), kind=kOutput, calls=%fused_computation.11 | convolution fusion | flops 2882906624 | bytes 16837312 | tf_op jit(solution)/shard_map/dot_general | solution.py:72
  326.2 9.9 %psum.43 = bf16[2,2048]{1,0:T(2,128)(2,1)S(1)} all-reduce(bf16[2,2048]{1,0:T(2,128)(2,1)S(1)} %pad_maximum_fusion.4), channel_id=1, replica_groups=mesh['fsdp'=2,'heads'=4,'tensor'=4] {'tensor'}, use_global_device_ids=true, to_apply=%region_9.10 | all-reduce | flops 4096 | bytes 16384 | tf_op jit(solution)/shard_map/psum | solution.py:82
  336.3 12.9 %convert_reduce_fusion.2 = (f32[684]{0:T(1024)S(1)}, bf16[2048,684]{0,1:T(8,128)(2,1)}, f32[684]{0:T(1024)S(1)}, bf16[2048,684]{0,1:T(8,128)(2,1)}) fusion(f32[2048,684]{0,1:T(8,128)} %copy-done.19, f32[684]{0:T(1024)S(1)} %convert_element_type.486, f32[2048]{0:T(1024)S(1)} %bitcast.246, f32[2048]{0:T(1024)S(1)} %add_rsqrt_fusion, ...), kind=kLoop, calls=%fused_computation.12 | loop fusion | flops 40622760 | bytes 28065824 | tf_op jit(solution)/shard_map/reduce_sum | solution.py:337
  349.2 23.9 %reduce-scatter.19.cloned.1.call-done = bf16[128,684]{1,0:T(8,128)(2,1)} async-done(((bf16[1024,684]{1,0:T(8,128)(2,1)}), bf16[128,684]{1,0:T(8,128)(2,1)}) %reduce-scatter.19.cloned.1.call-update) | async-done | bytes 175120
  374.2 5.9 fusion.67
  380.1 5.3 add_convert_fusion
  385.4 7.3 %convolution_convert_fusion.3 = bf16[1024,684]{0,1:T(8,128)(2,1)} fusion(bf16[2048,1024]{1,0:T(8,128)(2,1)} %bitcast.254, bf16[2048,684]{0,1:T(8,128)(2,1)} %get-tuple-element.94), kind=kOutput, calls=%fused_computation.77 | convolution fusion | flops 2869604352 | bytes 8396800 | tf_op jit(solution)/shard_map/dot_general | solution.py:66
  395.7 7.3 %convolution_convert_fusion.4 = bf16[1024,684]{0,1:T(8,128)(2,1)} fusion(bf16[2048,1024]{1,0:T(8,128)(2,1)} %bitcast.255, bf16[2048,684]{0,1:T(8,128)(2,1)} %get-tuple-element.54), kind=kOutput, calls=%fused_computation.78 | convolution fusion | flops 2869604352 | bytes 8396800 | tf_op jit(solution)/shard_map/dot_general | solution.py:66
  405.5 25.4 %all-reduce.9 = (f32[684]{0:T(1024)}, f32[684]{0:T(1024)}, f32[684]{0:T(1024)}, f32[684]{0:T(1024)}) all-reduce(f32[684]{0:T(1024)S(1)} %get-tuple-element.102, f32[684]{0:T(1024)S(1)} %get-tuple-element.93, f32[684]{0:T(1024)S(1)} %get-tuple-element.63, ...), channel_id=1, replica_groups=mesh['fsdp'=2,'heads'=4,'tensor'=4] {'fsdp','heads'}, use_global_device_ids=true, to_apply=%region_13.14 | all-reduce | flops 2736 | bytes 21888 | tf_op jit(solution)/shard_map/psum | solution.py:548
  430.9 31.5 %reduce-scatter.13.cloned.1.call-done = bf16[2,256,1024]{2,1,0:T(8,128)(2,1)} async-done(((bf16[8,256,1024]{2,1,0:T(8,128)(2,1)}), bf16[2,256,1024]{2,1,0:T(8,128)(2,1)}) %reduce-scatter.13.cloned.1.call-update) | async-done | bytes 1048592 | tf_op jit(solution)/shard_map/reduce_scatter | solution.py:163
  474.7 5.8 convolution_convert_fusion
  486.2 4.4 collective-permute-start.14
  496.5 46.3 %shard_map.374 = bf16[4,2,256,768]{3,2,1,0:T(8,128)(2,1)S(1)} custom-call(bf16[4,2,256,768]{3,2,1,0:T(8,128)(2,1)} %bitcast.200, bf16[4,2,256,256]{3,2,1,0:T(8,128)(2,1)S(1)} %copy-done.1, f32[1024,128]{1,0:T(8,128)S(1)} %copy-done.5, f32[1024,128]{1,0:T(8,128)S(1)} %copy-done.3), custom_call_target="tpu_custom_call" | custom-call | flops 10737418240 | bytes 8388608 | tf_op jit(solution)/shard_map/pallas_call | solution.py:268
  553.9 7.7 %fusion.56 = (bf16[1024]{0:T(1024)(128)(2,1)S(1)}, bf16[1024]{0:T(1024)(128)(2,1)S(1)}, bf16[2048,1024]{1,0:T(8,128)(2,1)}) fusion(f32[2048]{0:T(1024)S(1)} %bitcast.249, f32[2048]{0:T(1024)S(1)} %bitcast.248, bf16[2,2,2,256,1024]{4,3,2,1,0:T(8,128)(2,1)} %get-tuple-element.101, bf16[2048,768]{1,0:T(8,128)(2,1)S(1)} %bitcast.198, ...), kind=kOutput, calls=%fused_computation.191 | convolution fusion | flops 3235903488 | bytes 13127680 | tf_op jit(solution)/shard_map/dot_general | solution.py:72
  565.0 4.5 constant_dynamic-slice_fusion
  578.8 5.6 collective-permute-start.16
  585.2 7.2 %collective-permute-done.22 = bf16[576,768]{1,0:T(8,128)(2,1)} collective-permute-done((bf16[576,768]{1,0:T(8,128)(2,1)}, bf16[576,768]{1,0:T(8,128)(2,1)}, u32[]{:S(2)}, u32[]{:S(2)}) %collective-permute-start.22) | collective-permute-done | bytes 884768 | tf_op jit(solution)/shard_map/ppermute | solution.py:116
  594.8 15.9 %collective-permute-done.16 = bf16[2,256,1024]{2,1,0:T(8,128)(2,1)} collective-permute-done((bf16[2,256,1024]{2,1,0:T(8,128)(2,1)}, bf16[2,256,1024]{2,1,0:T(8,128)(2,1)}, u32[]{:S(2)}, u32[]{:S(2)}) %collective-permute-start.16) | collective-permute-done | bytes 1048608 | tf_op jit(solution)/shard_map/ppermute | solution.py:158
  610.7 4.1 fusion.17
  621.3 6.1 collective-permute-start.17
  635.5 6.5 reduce-scatter.15.cloned.1.call-done
  643.7 3.7 all-to-all-start.3
  647.4 4.8 collective-permute-done.18
  656.3 5.8 all-to-all-done.3
  671.2 3.9 fusion.11
  675.1 6.9 collective-permute-done.19
  682.1 3.6 fusion.22
  (362 shorter events, 163.6 us)
Async XLA Ops:
  7.2 39.3 %copy-start.11 = (bf16[2,256,1024]{2,1,0:T(8,128)(2,1)S(1)}, bf16[2,256,1024]{2,1,0:T(8,128)(2,1)}, u32[]{:S(2)}) copy-start(bf16[2,256,1024]{2,1,0:T(8,128)(2,1)} %param.22) | copy-start | bytes 3145732
  7.2 74.1 %all-gather.18.cloned.1.call-start = ((), (), s32[]{:S(2)}) async-start(), calls=%async_computation.18 | async-start | bytes 1880064 | tf_op jit(solution)/shard_map/all_gather | solution.py:418
  22.5 159.7 %all-gather.8.cloned.1.call-start = ((), (), s32[]{:S(2)}) async-start(), calls=%async_computation.10 | async-start | bytes 2359296 | tf_op jit(solution)/shard_map/all_gather | solution.py:441
  22.6 5.4 collective-permute-start.8
  26.1 6.2 collective-permute-start.11
  27.9 6.8 collective-permute-start.9
  32.2 7.1 %collective-permute-start.12 = (bf16[32,1024]{1,0:T(8,128)(2,1)S(1)}, bf16[32,1024]{1,0:T(8,128)(2,1)S(1)}, u32[]{:S(2)}, u32[]{:S(2)}) collective-permute-start(bf16[32,1024]{1,0:T(8,128)(2,1)S(1)} %collective-permute-done.11), channel_id=1, source_target_pairs={{1,0},{2,1},{3,2},{5,4},{6,5},{7,6},{9,8},{10,9},{11,10},{13,12},{... | collective-permute-start | bytes 196616 | tf_op jit(solution)/shard_map/ppermute | solution.py:129
  34.8 7.0 %collective-permute-start.10 = (bf16[32,1024]{1,0:T(8,128)(2,1)S(1)}, bf16[32,1024]{1,0:T(8,128)(2,1)S(1)}, u32[]{:S(2)}, u32[]{:S(2)}) collective-permute-start(bf16[32,1024]{1,0:T(8,128)(2,1)S(1)} %collective-permute-done.9), channel_id=1, source_target_pairs={{0,1},{1,2},{2,3},{4,5},{5,6},{6,7},{8,9},{9,10},{10,11},{12,13},{... | collective-permute-start | bytes 196616 | tf_op jit(solution)/shard_map/ppermute | solution.py:128
  39.3 6.4 collective-permute-start.13
  41.8 28.6 %copy-start.56 = (s32[2]{0:T(128)S(1)}, s32[2]{0:T(128)}, u32[]{:S(2)}) copy-start(s32[2]{0:T(128)} %param.23) | copy-start | bytes 28
  46.4 141.5 %all-gather.10.cloned.1.call-start = ((), (), s32[]{:S(2)}) async-start(), calls=%async_computation.11 | async-start | bytes 1585152 | tf_op jit(solution)/shard_map/all_gather | solution.py:451
  46.5 22.2 %collective-permute-start = (bf16[1,1,2,256,1024]{4,3,2,1,0:T(8,128)(2,1)S(1)}, bf16[1,1,2,256,1024]{4,3,2,1,0:T(8,128)(2,1)S(1)}, u32[]{:S(2)}, u32[]{:S(2)}) collective-permute-start(bf16[1,1,2,256,1024]{4,3,2,1,0:T(8,128)(2,1)S(1)} %bitcast.201), channel_id=1, source_target_pairs={{0,8},{4,12},{8,0},{12,4},{1,9},{5,13},{9,1},{13,5},{2,10},{6,14},... | collective-permute-start | bytes 3145736 | tf_op jit(solution)/shard_map/ppermute | solution.py:97
  70.4 13.6 %collective-permute-start.1 = (bf16[2,1,2,256,1024]{4,3,2,1,0:T(8,128)(2,1)}, bf16[2,1,2,256,1024]{4,3,2,1,0:T(8,128)(2,1)}, u32[]{:S(2)}, u32[]{:S(2)}) collective-permute-start(bf16[2,1,2,256,1024]{4,3,2,1,0:T(8,128)(2,1)} %maximum_select_fusion.1), channel_id=1, source_target_pairs={{0,4},{4,0},{8,12},{12,8},{1,5},{5,1},{9,13},{13,9},{2,6},{6,2},{1... | collective-permute-start | bytes 6291464 | tf_op jit(solution)/shard_map/ppermute | solution.py:97
  70.4 394.5 %copy-start.45 = (f32[2]{0:T(128)}, f32[2]{0:T(128)S(1)}, u32[]{:S(2)}) copy-start(f32[2]{0:T(128)S(1)} %convert_element_type.460) | copy-start | bytes 28
  70.9 27.8 %collective-permute-start.5 = (bf16[2,256,1024]{2,1,0:T(8,128)(2,1)S(1)}, bf16[2,256,1024]{2,1,0:T(8,128)(2,1)}, u32[]{:S(2)}, u32[]{:S(2)}) collective-permute-start(bf16[2,256,1024]{2,1,0:T(8,128)(2,1)S(1)} %get-tuple-element.90), channel_id=1, source_target_pairs={{1,0},{2,1},{3,2},{5,4},{6,5},{7,6},{9,8},{10,9},{11,10},{13,12},{... | collective-permute-start | bytes 3145736 | tf_op jit(solution)/shard_map/ppermute | solution.py:129
  72.2 27.6 %collective-permute-start.2 = (bf16[2,256,1024]{2,1,0:T(8,128)(2,1)S(1)}, bf16[2,256,1024]{2,1,0:T(8,128)(2,1)}, u32[]{:S(2)}, u32[]{:S(2)}) collective-permute-start(bf16[2,256,1024]{2,1,0:T(8,128)(2,1)S(1)} %get-tuple-element.90), channel_id=1, source_target_pairs={{0,1},{1,2},{2,3},{4,5},{5,6},{6,7},{8,9},{9,10},{10,11},{12,13},{... | collective-permute-start | bytes 3145736 | tf_op jit(solution)/shard_map/ppermute | solution.py:128
  78.9 58.1 %copy-start.2 = (f32[1024,128]{1,0:T(8,128)}, f32[1024,128]{1,0:T(8,128)S(1)}, u32[]{:S(2)}) copy-start(f32[1024,128]{1,0:T(8,128)S(1)} %copy.83.sine_ref) | copy-start | bytes 1572868
  81.3 55.7 %copy-start.4 = (f32[1024,128]{1,0:T(8,128)}, f32[1024,128]{1,0:T(8,128)S(1)}, u32[]{:S(2)}) copy-start(f32[1024,128]{1,0:T(8,128)S(1)} %copy.82.cosine_ref) | copy-start | bytes 1572868
  99.8 27.0 %collective-permute-start.3 = (bf16[2,256,1024]{2,1,0:T(8,128)(2,1)}, bf16[2,256,1024]{2,1,0:T(8,128)(2,1)}, u32[]{:S(2)}, u32[]{:S(2)}) collective-permute-start(bf16[2,256,1024]{2,1,0:T(8,128)(2,1)} %collective-permute-done.2), channel_id=1, source_target_pairs={{0,1},{1,2},{2,3},{4,5},{5,6},{6,7},{8,9},{9,10},{10,11},{12,13},{... | collective-permute-start | bytes 3145736 | tf_op jit(solution)/shard_map/ppermute | solution.py:128
  105.3 26.6 %collective-permute-start.6 = (bf16[2,256,1024]{2,1,0:T(8,128)(2,1)}, bf16[2,256,1024]{2,1,0:T(8,128)(2,1)}, u32[]{:S(2)}, u32[]{:S(2)}) collective-permute-start(bf16[2,256,1024]{2,1,0:T(8,128)(2,1)} %collective-permute-done.5), channel_id=1, source_target_pairs={{1,0},{2,1},{3,2},{5,4},{6,5},{7,6},{9,8},{10,9},{11,10},{13,12},{... | collective-permute-start | bytes 3145736 | tf_op jit(solution)/shard_map/ppermute | solution.py:129
  126.8 35.5 %collective-permute-start.4 = (bf16[2,256,1024]{2,1,0:T(8,128)(2,1)}, bf16[2,256,1024]{2,1,0:T(8,128)(2,1)S(1)}, u32[]{:S(2)}, u32[]{:S(2)}) collective-permute-start(bf16[2,256,1024]{2,1,0:T(8,128)(2,1)} %collective-permute-done.3), channel_id=1, source_target_pairs={{0,1},{1,2},{2,3},{4,5},{5,6},{6,7},{8,9},{9,10},{10,11},{12,13},{... | collective-permute-start | bytes 3145736 | tf_op jit(solution)/shard_map/ppermute | solution.py:128
  131.8 31.4 %collective-permute-start.7 = (bf16[2,256,1024]{2,1,0:T(8,128)(2,1)}, bf16[2,256,1024]{2,1,0:T(8,128)(2,1)}, u32[]{:S(2)}, u32[]{:S(2)}) collective-permute-start(bf16[2,256,1024]{2,1,0:T(8,128)(2,1)} %collective-permute-done.6), channel_id=1, source_target_pairs={{1,0},{2,1},{3,2},{5,4},{6,5},{7,6},{9,8},{10,9},{11,10},{13,12},{... | collective-permute-start | bytes 3145736 | tf_op jit(solution)/shard_map/ppermute | solution.py:129
  163.2 17.9 %all-to-all-start.1 = ((bf16[4,2,256,256]{3,2,1,0:T(8,128)(2,1)}), bf16[4,2,256,256]{3,2,1,0:T(8,128)(2,1)S(1)}, u32[]{:S(2)}, u32[]{:S(2)}) async-start(bf16[4,2,256,256]{3,2,1,0:T(8,128)(2,1)} %shard_map.373), calls=%async_computation.1 | async-start | bytes 2097152 | tf_op jit(solution)/shard_map/all_to_all | solution.py:478
  166.7 31.3 %all-gather.12.cloned.1.call-start = ((), (), s32[]{:S(2)}) async-start(), calls=%async_computation.12 | async-start | bytes 1585152 | tf_op jit(solution)/shard_map/all_gather | solution.py:452
  167.3 113.5 %all-gather.14.cloned.1.call-start = ((), (), s32[]{:S(2)}) async-start(), calls=%async_computation.13 | async-start | bytes 5242880 | tf_op jit(solution)/shard_map/all_gather | solution.py:78
  186.1 278.9 %copy-start.7 = (f32[2,256,1024]{2,1,0:T(8,128)}, f32[2,256,1024]{2,1,0:T(8,128)S(1)}, u32[]{:S(2)}) copy-start(f32[2,256,1024]{2,1,0:T(8,128)S(1)} %get-tuple-element.99) | copy-start | bytes 6291460
  198.0 117.4 %all-gather.16.cloned.1.call-start = ((), (), s32[]{:S(2)}) async-start(), calls=%async_computation.14 | async-start | bytes 1585152 | tf_op jit(solution)/shard_map/all_gather | solution.py:453
  198.6 174.4 %reduce-scatter.19.cloned.1.call-start = ((), (), s32[]{:S(2)}) async-start(), calls=%async_computation.19 | async-start | bytes 1769472
  336.2 126.1 %reduce-scatter.13.cloned.1.call-start = ((), (), s32[]{:S(2)}) async-start(), calls=%async_computation.15 | async-start | bytes 5242880 | tf_op jit(solution)/shard_map/reduce_scatter | solution.py:163
  385.4 232.2 %reduce-scatter.23.cloned.1.call-start = ((), (), s32[]{:S(2)}) async-start(), calls=%async_computation.21 | async-start | bytes 1769472
  395.3 224.1 %reduce-scatter.21.cloned.1.call-start = ((), (), s32[]{:S(2)}) async-start(), calls=%async_computation.20 | async-start | bytes 1769472
  471.1 21.0 %all-to-all-start.2 = ((bf16[4,2,256,256]{3,2,1,0:T(8,128)(2,1)}), bf16[4,2,256,256]{3,2,1,0:T(8,128)(2,1)S(1)}, u32[]{:S(2)}, u32[]{:S(2)}) async-start(bf16[4,2,256,256]{3,2,1,0:T(8,128)(2,1)} %bitcast.195), calls=%async_computation.3 | async-start | bytes 2097152 | tf_op jit(solution)/shard_map/all_to_all | solution.py:560
  474.6 152.7 %reduce-scatter.17.cloned.1.call-start = ((), (), s32[]{:S(2)}) async-start(), calls=%async_computation.17 | async-start | bytes 327680 | tf_op jit(solution)/shard_map/reduce_scatter | solution.py:646
  483.0 59.8 %collective-permute-start.23 = (bf16[512,1024]{1,0:T(8,128)(2,1)}, bf16[512,1024]{1,0:T(8,128)(2,1)}, u32[]{:S(2)}, u32[]{:S(2)}) collective-permute-start(bf16[512,1024]{1,0:T(8,128)(2,1)} %dynamic-slice_bitcast_fusion.1), channel_id=1, source_target_pairs={{0,16},{16,0},{1,17},{17,1},{2,18},{18,2},{3,19},{19,3},{4,20},{20... | collective-permute-start | bytes 3145736 | tf_op jit(solution)/shard_map/ppermute | solution.py:116
  486.2 60.1 %collective-permute-start.14 = (bf16[2,256,1024]{2,1,0:T(8,128)(2,1)}, bf16[2,256,1024]{2,1,0:T(8,128)(2,1)}, u32[]{:S(2)}, u32[]{:S(2)}) collective-permute-start(bf16[2,256,1024]{2,1,0:T(8,128)(2,1)} %get-tuple-element.56), channel_id=1, source_target_pairs={{0,1},{1,2},{2,3},{4,5},{5,6},{6,7},{8,9},{9,10},{10,11},{12,13},{... | collective-permute-start | bytes 3145736 | tf_op jit(solution)/shard_map/ppermute | solution.py:158
  490.6 55.6 %collective-permute-start.15 = (bf16[2,256,1024]{2,1,0:T(8,128)(2,1)}, bf16[2,256,1024]{2,1,0:T(8,128)(2,1)}, u32[]{:S(2)}, u32[]{:S(2)}) collective-permute-start(bf16[2,256,1024]{2,1,0:T(8,128)(2,1)} %get-tuple-element.57), channel_id=1, source_target_pairs={{1,0},{2,1},{3,2},{5,4},{6,5},{7,6},{9,8},{10,9},{11,10},{13,12},{... | collective-permute-start | bytes 3145736 | tf_op jit(solution)/shard_map/ppermute | solution.py:158
  496.5 46.3 %copy-start.31 = (bf16[1024,1024]{1,0:T(8,128)(2,1)S(1)}, bf16[1024,1024]{1,0:T(8,128)(2,1)}, u32[]{:S(2)}) copy-start(bf16[1024,1024]{1,0:T(8,128)(2,1)} %copy-done.30) | copy-start | bytes 6291460
  546.3 26.4 %collective-permute-start.24 = (bf16[2,128,1024]{2,1,0:T(8,128)(2,1)}, bf16[2,128,1024]{2,1,0:T(8,128)(2,1)}, u32[]{:S(2)}, u32[]{:S(2)}) collective-permute-start(bf16[2,128,1024]{2,1,0:T(8,128)(2,1)} %dynamic-slice_bitcast_fusion.4), channel_id=1, source_target_pairs={{0,4},{4,0},{8,12},{12,8},{1,5},{5,1},{9,13},{13,9},{2,6},{6,2},{1... | collective-permute-start | bytes 1572872 | tf_op jit(solution)/shard_map/ppermute | solution.py:116
  570.5 22.0 %collective-permute-start.22 = (bf16[576,768]{1,0:T(8,128)(2,1)}, bf16[576,768]{1,0:T(8,128)(2,1)}, u32[]{:S(2)}, u32[]{:S(2)}) collective-permute-start(bf16[576,768]{1,0:T(8,128)(2,1)} %bitcast.196), channel_id=1, source_target_pairs={{0,16},{16,0},{1,17},{17,1},{2,18},{18,2},{3,19},{19,3},{4,20},{20... | collective-permute-start | bytes 2654216 | tf_op jit(solution)/shard_map/ppermute | solution.py:116
  572.6 56.2 %collective-permute-start.20 = (bf16[2,2,256,1024]{3,2,1,0:T(8,128)(2,1)}, bf16[2,2,256,1024]{3,2,1,0:T(8,128)(2,1)}, u32[]{:S(2)}, u32[]{:S(2)}) collective-permute-start(bf16[2,2,256,1024]{3,2,1,0:T(8,128)(2,1)} %dynamic-slice_bitcast_fusion), channel_id=1, source_target_pairs={{0,4},{4,0},{8,12},{12,8},{1,5},{5,1},{9,13},{13,9},{2,6},{6,2},{1... | collective-permute-start | bytes 6291464 | tf_op jit(solution)/shard_map/ppermute | solution.py:116
  573.9 10.5 %collective-permute-start.25 = (bf16[128,1024]{1,0:T(8,128)(2,1)S(1)}, bf16[128,1024]{1,0:T(8,128)(2,1)S(1)}, u32[]{:S(2)}, u32[]{:S(2)}) collective-permute-start(bf16[128,1024]{1,0:T(8,128)(2,1)S(1)} %fusion.30), channel_id=1, source_target_pairs={{0,8},{4,12},{8,0},{12,4},{1,9},{5,13},{9,1},{13,5},{2,10},{6,14},... | collective-permute-start | bytes 786440 | tf_op jit(solution)/shard_map/ppermute | solution.py:116
  578.8 31.9 %collective-permute-start.16 = (bf16[2,256,1024]{2,1,0:T(8,128)(2,1)}, bf16[2,256,1024]{2,1,0:T(8,128)(2,1)}, u32[]{:S(2)}, u32[]{:S(2)}) collective-permute-start(bf16[2,256,1024]{2,1,0:T(8,128)(2,1)} %fusion.16), channel_id=1, source_target_pairs={{0,1},{1,2},{2,3},{4,5},{5,6},{6,7},{8,9},{9,10},{10,11},{12,13},{... | collective-permute-start | bytes 3145736 | tf_op jit(solution)/shard_map/ppermute | solution.py:158
  585.2 56.8 %reduce-scatter.15.cloned.1.call-start = ((), (), s32[]{:S(2)}) async-start(), calls=%async_computation.16 | async-start | bytes 1105920 | tf_op jit(solution)/shard_map/reduce_scatter | solution.py:629
  614.8 37.4 %collective-permute-start.18 = (bf16[2,256,1024]{2,1,0:T(8,128)(2,1)S(1)}, bf16[2,256,1024]{2,1,0:T(8,128)(2,1)S(1)}, u32[]{:S(2)}, u32[]{:S(2)}) collective-permute-start(bf16[2,256,1024]{2,1,0:T(8,128)(2,1)S(1)} %get-tuple-element.61), channel_id=1, source_target_pairs={{1,0},{2,1},{3,2},{5,4},{6,5},{7,6},{9,8},{10,9},{11,10},{13,12},{... | collective-permute-start | bytes 3145736 | tf_op jit(solution)/shard_map/ppermute | solution.py:158
  621.3 53.9 %collective-permute-start.17 = (bf16[2,256,1024]{2,1,0:T(8,128)(2,1)}, bf16[2,256,1024]{2,1,0:T(8,128)(2,1)}, u32[]{:S(2)}, u32[]{:S(2)}) collective-permute-start(bf16[2,256,1024]{2,1,0:T(8,128)(2,1)} %get-tuple-element.60), channel_id=1, source_target_pairs={{0,1},{1,2},{2,3},{4,5},{5,6},{6,7},{8,9},{9,10},{10,11},{12,13},{... | collective-permute-start | bytes 3145736 | tf_op jit(solution)/shard_map/ppermute | solution.py:158
  635.1 33.1 %collective-permute-start.21 = (bf16[2,256,1024]{2,1,0:T(8,128)(2,1)}, bf16[2,256,1024]{2,1,0:T(8,128)(2,1)}, u32[]{:S(2)}, u32[]{:S(2)}) collective-permute-start(bf16[2,256,1024]{2,1,0:T(8,128)(2,1)} %fusion.27), channel_id=1, source_target_pairs={{0,8},{4,12},{8,0},{12,4},{1,9},{5,13},{9,1},{13,5},{2,10},{6,14},... | collective-permute-start | bytes 3145736 | tf_op jit(solution)/shard_map/ppermute | solution.py:116
  643.7 18.4 %all-to-all-start.3 = ((bf16[4,36,768]{2,1,0:T(8,128)(2,1)}), bf16[4,36,768]{2,1,0:T(8,128)(2,1)S(1)}, u32[]{:S(2)}, u32[]{:S(2)}) async-start(bf16[4,36,768]{2,1,0:T(8,128)(2,1)} %all_to_all.18), calls=%async_computation.5 | async-start | bytes 491520 | tf_op jit(solution)/shard_map/all_to_all | solution.py:630
  654.8 27.2 %collective-permute-start.19 = (bf16[2,256,1024]{2,1,0:T(8,128)(2,1)}, bf16[2,256,1024]{2,1,0:T(8,128)(2,1)}, u32[]{:S(2)}, u32[]{:S(2)}) collective-permute-start(bf16[2,256,1024]{2,1,0:T(8,128)(2,1)} %fusion.15), channel_id=1, source_target_pairs={{1,0},{2,1},{3,2},{5,4},{6,5},{7,6},{9,8},{10,9},{11,10},{13,12},{... | collective-permute-start | bytes 3145736 | tf_op jit(solution)/shard_map/ppermute | solution.py:158
  (50 other events, 421.2 us)
Sparse Core Ops, SparseCore 0:
  22.6 46.1 all-gather.17
  71.3 26.1 all-gather.7
  99.4 25.0 all-gather.9
  169.1 28.8 all-gather.11
  200.0 80.7 all-gather.13
  282.5 23.5 all-gather.15
  336.3 36.6 reduce-scatter.18
  385.5 76.7 reduce-scatter.12
  465.6 45.3 reduce-scatter.22
  514.1 38.4 reduce-scatter.20
  585.3 21.7 reduce-scatter.16
  609.2 32.6 reduce-scatter.14
where the time goes:
time: 701 us; the launch traced here: 693 us
  waiting for transfers between devices  239 us (34%)
  other arithmetic  83.2 us (12%)
  matrix products  80.2 us (11%)
  local copies, waits for them, and re-layouts  75.4 us (11%)
  starting transfers between devices  72.5 us (10%)
  Pallas kernels  71.5 us (10%)
  blocking collectives  54.7 us (8%)
  between operations  15.9 us (2%)
    pallas_call x2, Pallas kernels, attention_call(): pl.pallas_call(kernel, grid=(seq_count, pair_count), in_specs=[per_pair(3...  71.5 us
    all_gather x1, waiting for transfers between devices, gather_rows(): return lax.all_gather(block_values, 'tensor', axis=0, tiled=True)  71.5 us
    unnamed x144, local copies, waits for them, and re-layouts  32 us
    reduce_scatter x1, waiting for transfers between devices, scatter_rows(): lax.psum_scatter(term_fn(jnp.int32(0), row_total * lax.axis_size('tensor'...  31.5 us
    dot_general x5, matrix products, times_transpose(): lax.dot_general(left_rows, right_rows, (((1,), (1,)), ((), ())), preferre...  30.9 us
    ppermute x6, waiting for transfers between devices, line_scatter_step(): passed.append(lax.ppermute(gated, axis_name, pairs[side]))  27.7 us
    ppermute x6, starting transfers between devices, line_step(): below.append(lax.ppermute(below[-1], axis_name, upward))  27.5 us
    psum x1, blocking collectives, on_device(): lax.psum((vector_grads[0], vector_grads[1], vector_grads[2], vector_grads...  25.4 us
  transfers between devices with their start and end apart: 41, of which 21 were waited for; matrix products, arithmetic and copies ran while one was open for 28% of the time, Pallas kernels for 10%

commit v1 on v0

--- a/solution.py
+++ b/solution.py
@@ -8,6 +8,7 @@
 from jax.sharding import PartitionSpec as P
 
 
+FSDP, HEADS, TENSOR = "fsdp", "heads", "tensor"
 HD = 64
 PAIR = 2 * HD
 FF_REAL = 2730
@@ -75,11 +76,11 @@
 
 
 def gather_rows(block_values):
-    return lax.all_gather(block_values, "tensor", axis=0, tiled=True)
+    return lax.all_gather(block_values, TENSOR, axis=0, tiled=True)
 
 
 def tensor_sums(first_sum, second_sum):
-    both = lax.psum(jnp.stack([first_sum, second_sum]).astype(jnp.bfloat16), "tensor")
+    both = lax.psum(jnp.stack([first_sum, second_sum]).astype(jnp.bfloat16), TENSOR)
     return (both[0].astype(jnp.float32), both[1].astype(jnp.float32))
 
 
@@ -161,8 +162,8 @@
 
 def scatter_rows(term_fn, row_total):
     return lax.psum_scatter(
-        term_fn(jnp.int32(0), row_total * lax.axis_size("tensor")).astype(jnp.bfloat16),
-        "tensor",
+        term_fn(jnp.int32(0), row_total * lax.axis_size(TENSOR)).astype(jnp.bfloat16),
+        TENSOR,
         scatter_dimension=0,
         tiled=True,
     ).astype(jnp.float32)
@@ -365,21 +366,21 @@
     down_bias,
 ):
     seq_local, piece_len, width = inputs.shape
-    head_ways = lax.axis_size("heads")
+    head_ways = lax.axis_size(HEADS)
     group_width = width // head_ways
     group_pairs = group_width // PAIR
     token_count = seq_local * piece_len
-    fsdp_ways, tensor_ways = lax.axis_size("fsdp"), lax.axis_size("tensor")
+    fsdp_ways, tensor_ways = lax.axis_size(FSDP), lax.axis_size(TENSOR)
     row_part = query_weight.shape[0]
-    group_index = lax.axis_index("heads")
-    inputs_group = cube_gather(inputs, "heads")
+    group_index = lax.axis_index(HEADS)
+    inputs_group = cube_gather(inputs, HEADS)
     grad_flags = slot_flag.astype(jnp.float32)[:, None, None]
     grad_total = grad_flags * cotangent.astype(jnp.float32)
     grad_branch = grad_total.astype(jnp.bfloat16)
     below, above = [grad_branch], [grad_branch]
-    line_step(below, above, "tensor")
+    line_step(below, above, TENSOR)
     below[-1], above[-1] = after(below[-1], inputs_group), after(above[-1], inputs_group)
-    line_step(below, above, "tensor")
+    line_step(below, above, TENSOR)
     stacked = jnp.stack(
         [
             member.reshape(row_part, head_ways, group_pairs, PAIR)
@@ -413,10 +414,10 @@
         axis=1,
     )
     own_columns = lax.all_to_all(
-        sent_columns, "heads", split_axis=0, concat_axis=0, tiled=True
+        sent_columns, HEADS, split_axis=0, concat_axis=0, tiled=True
     )
     columns = lax.all_gather(
-        own_columns.reshape(-1, 3 * group_width), ("fsdp", "tensor"), axis=0, tiled=True
+        own_columns.reshape(-1, 3 * group_width), (FSDP, TENSOR), axis=0, tiled=True
     )
     group_f = inputs_group.reshape(-1, width).astype(jnp.float32)
     group_mean = jnp.mean(group_f, axis=-1, keepdims=True)
@@ -428,7 +429,7 @@
     ).transpose(0, 2, 1, 3, 4)
     qkv_part = columns[:, :, :, :row_part].reshape(width, 3 * group_width)
     below[-1], above[-1] = after(below[-1], columns), after(above[-1], columns)
-    line_step(below, above, "tensor")
+    line_step(below, above, TENSOR)
     gathered = (
         columns[:, :, :, row_part, : len(vectors) * row_part]
         .reshape(-1, 8, row_part)
@@ -437,10 +438,10 @@
     )
     out_below, out_above = [out_weight], [out_weight]
     for _ in range(tensor_ways - 1):
-        line_step(out_below, out_above, "tensor")
+        line_step(out_below, out_above, TENSOR)
     out_full = lax.all_gather(
-        line_pick(out_below, out_above, "tensor"),
-        ("fsdp", "heads"),
+        line_pick(out_below, out_above, TENSOR),
+        (FSDP, HEADS),
         axis=0,
         tiled=True,
     )
@@ -448,9 +449,9 @@
         member.astype(jnp.float32) for member in gathered
     ]
     gate_part, up_part, down_part = (
-        lax.all_gather(gate_weight, ("fsdp", "heads"), axis=0, tiled=True),
-        lax.all_gather(up_weight, ("fsdp", "heads"), axis=0, tiled=True),
-        lax.all_gather(down_weight, ("fsdp", "heads"), axis=1, tiled=True),
+        lax.all_gather(gate_weight, (FSDP, HEADS), axis=0, tiled=True),
+        lax.all_gather(up_weight, (FSDP, HEADS), axis=0, tiled=True),
+        lax.all_gather(down_weight, (FSDP, HEADS), axis=1, tiled=True),
     )
     inputs_f = inputs.astype(jnp.float32)
     _, unit_one, inv_one = layer_norm(inputs_f, gain_one, shift_one)
@@ -474,9 +475,9 @@
         (mixed_heads, below[-1], above[-1])
     )
     for _ in range(tensor_ways - 4):
-        line_step(below, above, "tensor")
-    mixed_parts = lax.all_to_all(mixed_heads, "heads", split_axis=0, concat_axis=0, tiled=True)
-    grad_rows = line_pick(below, above, "tensor").reshape(-1, width)
+        line_step(below, above, TENSOR)
+    mixed_parts = lax.all_to_all(mixed_heads, HEADS, split_axis=0, concat_axis=0, tiled=True)
+    grad_rows = line_pick(below, above, TENSOR).reshape(-1, width)
     mixed_flat = mixed_parts.transpose(1, 2, 0, 3).reshape(token_count, width)
     residual = inputs_f + (
         jnp.dot(mixed_flat, out_full, preferred_element_type=jnp.float32) + out_shift
@@ -488,7 +489,7 @@
     ffn_local = gate_part.shape[1]
     token_rows3 = gather_rows(after(low_two, gate_part, up_part, below[-1], above[-1]))
     token_rows = token_rows3.reshape(-1, width)
-    col_index = lax.axis_index("tensor") * ffn_local + jnp.arange(ffn_local, dtype=jnp.int32)
+    col_index = lax.axis_index(TENSOR) * ffn_local + jnp.arange(ffn_local, dtype=jnp.int32)
     unit_mask = (col_index < FF_REAL).astype(jnp.float32)
     gate_pre, up_pre, hidden = hidden_forward(
         token_rows,
@@ -513,7 +514,7 @@
 
     down_grad = outer_product(normed_hidden, grad_rows)
     down_weight_grad = lax.psum_scatter(
-        down_grad.astype(jnp.bfloat16), ("fsdp", "heads"), scatter_dimension=1, tiled=True
+        down_grad.astype(jnp.bfloat16), (FSDP, HEADS), scatter_dimension=1, tiled=True
     )
     grad_normed = times_transpose(after(grad_rows, down_grad), down_part)
     scaled, scaled_sum, cross_sum = hidden_backward_terms(
@@ -538,15 +539,15 @@
     grad_normed_two = scatter_rows(input_term, seq_local)
     gate_weight_grad, up_weight_grad = (
         lax.psum_scatter(
-            gate_grad.astype(jnp.bfloat16), ("fsdp", "heads"), scatter_dimension=0, tiled=True
+            gate_grad.astype(jnp.bfloat16), (FSDP, HEADS), scatter_dimension=0, tiled=True
         ).astype(jnp.float32),
         lax.psum_scatter(
-            up_grad.astype(jnp.bfloat16), ("fsdp", "heads"), scatter_dimension=0, tiled=True
+            up_grad.astype(jnp.bfloat16), (FSDP, HEADS), scatter_dimension=0, tiled=True
         ).astype(jnp.float32),
     )
     down_weight_grad = down_weight_grad.astype(jnp.float32)
     gate_bias_grad, up_bias_grad, inner_gain_grad, inner_shift_grad = lax.psum(
-        (vector_grads[0], vector_grads[1], vector_grads[2], vector_grads[3]), ("fsdp", "heads")
+        (vector_grads[0], vector_grads[1], vector_grads[2], vector_grads[3]), (FSDP, HEADS)
     )
     grad_normed_two = after(grad_normed_two, gate_bias_grad)
     grad_residual = grad_total + norm_backward(grad_normed_two, unit_two, inv_two, gain_two)
@@ -558,17 +559,18 @@
     grad_mixed = times_transpose(grad_attn, out_full).astype(jnp.bfloat16)
     grad_parts = grad_mixed.reshape(seq_local, piece_len, head_ways, group_width)
     grad_heads = lax.all_to_all(
-        grad_parts.transpose(2, 0, 1, 3), "heads", split_axis=0, concat_axis=0, tiled=True
+        grad_parts.transpose(2, 0, 1, 3), HEADS, split_axis=0, concat_axis=0, tiled=True
     )
     branch_terms = down_term(seq_local * tensor_ways).astype(jnp.bfloat16)
     branch_terms = branch_terms.reshape((tensor_ways,) + inputs.shape)
-    running = line_scatter_step(branch_terms, None, tensor_ways - 1, "tensor", grad_mixed)
+    running = line_scatter_step(branch_terms, None, tensor_ways - 1, TENSOR, grad_mixed)
     qkv_grad = attend_backward(qkv_lin, grad_heads, tables)
     qkv_grad = after(qkv_grad, *running)
-    for distance in range(tensor_ways - 2, 0, -1):
-        running = line_scatter_step(branch_terms, running, distance, "tensor", qkv_grad)
+    running = line_scatter_step(branch_terms, running, tensor_ways - 2, TENSOR, qkv_grad)
+    for distance in range(tensor_ways - 3, 0, -1):
+        running = line_scatter_step(branch_terms, running, distance, TENSOR, qkv_grad)
     branch_out = (
-        line_term(branch_terms, 0, "tensor")
+        line_term(branch_terms, 0, TENSOR)
         + running[0].astype(jnp.float32)
         + running[1].astype(jnp.float32)
     )
@@ -579,7 +581,7 @@
     shift_one_grad = jnp.sum(group_grad, axis=0)
     group_terms = group_grad.astype(jnp.bfloat16)
     grad_normed_one = cube_scatter(
-        group_terms.reshape((head_ways,) + inputs.shape), "heads"
+        group_terms.reshape((head_ways,) + inputs.shape), HEADS
     )
     qkv_shift_grad = jnp.sum(qkv_grad, axis=0, dtype=jnp.float32).reshape(group_pairs, 3, PAIR)
 
@@ -624,11 +626,11 @@
     ).transpose(0, 2, 1, 3, 4)
     qkv_terms = jnp.concatenate([qkv_terms, vector_rows.astype(jnp.bfloat16)], axis=3)
     qkv_half = cube_scatter(
-        qkv_terms.reshape(fsdp_ways, -1, 3 * group_width), "fsdp"
+        qkv_terms.reshape(fsdp_ways, -1, 3 * group_width), FSDP
     ).astype(jnp.bfloat16)
-    qkv_rows = lax.psum_scatter(qkv_half, "tensor", scatter_dimension=0, tiled=True)
+    qkv_rows = lax.psum_scatter(qkv_half, TENSOR, scatter_dimension=0, tiled=True)
     qkv_columns = lax.all_to_all(
-        qkv_rows, "heads", split_axis=0, concat_axis=0, tiled=True
+        qkv_rows, HEADS, split_axis=0, concat_axis=0, tiled=True
     ).reshape(head_ways, row_part + extra_rows, 3 * group_width)
     qkv_weight_grads = (
         qkv_columns[:, :row_part]
@@ -641,10 +643,10 @@
         qkv_columns[:, row_part, :vector_lanes].astype(jnp.float32), axis=0
     ).reshape(-1, row_part)
     out_terms = out_weight_part.astype(jnp.bfloat16).reshape(fsdp_ways, -1, width)
-    out_half = cube_scatter(out_terms, "fsdp").astype(jnp.bfloat16)
-    out_eighth = cube_scatter(out_half.reshape(head_ways, -1, width), "heads")
+    out_half = cube_scatter(out_terms, FSDP).astype(jnp.bfloat16)
+    out_eighth = cube_scatter(out_half.reshape(head_ways, -1, width), HEADS)
     out_weight_grad = lax.psum_scatter(
-        out_eighth.astype(jnp.bfloat16), "tensor", scatter_dimension=0, tiled=True
+        out_eighth.astype(jnp.bfloat16), TENSOR, scatter_dimension=0, tiled=True
     ).astype(jnp.float32)
     attn_sums = tuple(qkv_weight_grads) + (out_weight_grad,) + tuple(own_sums)
     return (
@@ -677,51 +679,51 @@
         on_device,
         mesh=mesh,
         in_specs=(
-            P(("fsdp", "tensor"), "heads", None),
-            P(("fsdp", "tensor")),
-            P(("fsdp", "tensor"), "heads", None),
-            P(("fsdp", "heads", "tensor")),
-            P(("fsdp", "heads", "tensor")),
-            P(("fsdp", "heads", "tensor"), None),
-            P(("fsdp", "heads", "tensor")),
-            P(("fsdp", "heads", "tensor"), None),
-            P(("fsdp", "heads", "tensor"), None),
-            P(("fsdp", "heads", "tensor")),
-            P(("fsdp", "heads", "tensor"), None),
-            P(("fsdp", "heads", "tensor")),
-            P(("fsdp", "heads", "tensor")),
-            P(("fsdp", "heads", "tensor")),
-            P(("fsdp", "heads"), "tensor"),
-            P("tensor"),
-            P(("fsdp", "heads"), "tensor"),
-            P("tensor"),
-            P("tensor"),
-            P("tensor"),
-            P("tensor", ("fsdp", "heads")),
-            P(("fsdp", "heads", "tensor")),
+            P((FSDP, TENSOR), HEADS, None),
+            P((FSDP, TENSOR)),
+            P((FSDP, TENSOR), HEADS, None),
+            P((FSDP, HEADS, TENSOR)),
+            P((FSDP, HEADS, TENSOR)),
+            P((FSDP, HEADS, TENSOR), None),
+            P((FSDP, HEADS, TENSOR)),
+            P((FSDP, HEADS, TENSOR), None),
+            P((FSDP, HEADS, TENSOR), None),
+            P((FSDP, HEADS, TENSOR)),
+            P((FSDP, HEADS, TENSOR), None),
+            P((FSDP, HEADS, TENSOR)),
+            P((FSDP, HEADS, TENSOR)),
+            P((FSDP, HEADS, TENSOR)),
+            P((FSDP, HEADS), TENSOR),
+            P(TENSOR),
+            P((FSDP, HEADS), TENSOR),
+            P(TENSOR),
+            P(TENSOR),
+            P(TENSOR),
+            P(TENSOR, (FSDP, HEADS)),
+            P((FSDP, HEADS, TENSOR)),
         ),
         out_specs=(
-            P(("fsdp", "tensor"), "heads", None),
-            P(("fsdp", "tensor"), "heads", None),
-            P(("fsdp", "heads", "tensor")),
-            P(("fsdp", "heads", "tensor")),
-            P(("fsdp", "heads", "tensor"), None),
-            P(("fsdp", "heads", "tensor")),
-            P(("fsdp", "heads", "tensor"), None),
-            P(("fsdp", "heads", "tensor"), None),
-            P(("fsdp", "heads", "tensor")),
-            P(("fsdp", "heads", "tensor"), None),
-            P(("fsdp", "heads", "tensor")),
-            P(("fsdp", "heads", "tensor")),
-            P(("fsdp", "heads", "tensor")),
-            P(("fsdp", "heads"), "tensor"),
-            P("tensor"),
-            P(("fsdp", "heads"), "tensor"),
-            P("tensor"),
-            P("tensor"),
-            P("tensor"),
-            P("tensor", ("fsdp", "heads")),
-            P(("fsdp", "heads", "tensor")),
+            P((FSDP, TENSOR), HEADS, None),
+            P((FSDP, TENSOR), HEADS, None),
+            P((FSDP, HEADS, TENSOR)),
+            P((FSDP, HEADS, TENSOR)),
+            P((FSDP, HEADS, TENSOR), None),
+            P((FSDP, HEADS, TENSOR)),
+            P((FSDP, HEADS, TENSOR), None),
+            P((FSDP, HEADS, TENSOR), None),
+            P((FSDP, HEADS, TENSOR)),
+            P((FSDP, HEADS, TENSOR), None),
+            P((FSDP, HEADS, TENSOR)),
+            P((FSDP, HEADS, TENSOR)),
+            P((FSDP, HEADS, TENSOR)),
+            P((FSDP, HEADS), TENSOR),
+            P(TENSOR),
+            P((FSDP, HEADS), TENSOR),
+            P(TENSOR),
+            P(TENSOR),
+            P(TENSOR),
+            P(TENSOR, (FSDP, HEADS)),
+            P((FSDP, HEADS, TENSOR)),
         ),
         check_vma=False,
     )

time: 701 us -> 701 us (level)
  no operation moved by 1% of the time
where the time goes in v1:
time: 701 us; the launch traced here: 693 us
  waiting for transfers between devices  239 us (34%)
  other arithmetic  83.2 us (12%)
  matrix products  80.2 us (11%)
  local copies, waits for them, and re-layouts  75.4 us (11%)
  starting transfers between devices  72.5 us (10%)
  Pallas kernels  71.5 us (10%)
  blocking collectives  54.7 us (8%)
  between operations  15.9 us (2%)
    pallas_call x2, Pallas kernels, attention_call(): pl.pallas_call(kernel, grid=(seq_count, pair_count), in_specs=[per_pair(3...  71.5 us
    all_gather x1, waiting for transfers between devices, gather_rows(): return lax.all_gather(block_values, TENSOR, axis=0, tiled=True)  71.5 us
    unnamed x144, local copies, waits for them, and re-layouts  32 us
    reduce_scatter x1, waiting for transfers between devices, scatter_rows(): lax.psum_scatter(term_fn(jnp.int32(0), row_total * lax.axis_size(TENSOR))...  31.5 us
    dot_general x5, matrix products, times_transpose(): lax.dot_general(left_rows, right_rows, (((1,), (1,)), ((), ())), preferre...  30.9 us
    ppermute x6, waiting for transfers between devices, line_scatter_step(): passed.append(lax.ppermute(gated, axis_name, pairs[side]))  27.7 us
    ppermute x6, starting transfers between devices, line_step(): below.append(lax.ppermute(below[-1], axis_name, upward))  27.5 us
    psum x1, blocking collectives, on_device(): lax.psum((vector_grads[0], vector_grads[1], vector_grads[2], vector_grads...  25.4 us
  transfers between devices with their start and end apart: 41, of which 21 were waited for; matrix products, arithmetic and copies ran while one was open for 28% of the time, Pallas kernels for 10%

profile of v1, /device:TPU:0, one launch (start us, length us, event | category | flops | bytes accessed | tf_op | source)
XLA Modules:
  0.0 692.7 jit_solution(3502130643796988918)
XLA Ops:
  11.8 9.9 %all_to_all.24 = bf16[4,33,768]{2,1,0:T(8,128)(2,1)S(1)} all-to-all(bf16[4,33,768]{2,1,0:T(8,128)(2,1)S(1)} %pad_maximum_fusion.1), channel_id=1, replica_groups=mesh['fsdp'=2,'heads'=4,'tensor'=4] {'heads'}, dimensions={0} | all-to-all | bytes 405504 | tf_op jit(solution)/shard_map/all_to_all | solution.py:416
  27.9 4.3 collective-permute-start.9
  34.8 4.4 collective-permute-start.10
  41.8 3.9 collective-permute-done.13
  47.5 21.3 %collective-permute-done = bf16[1,1,2,256,1024]{4,3,2,1,0:T(8,128)(2,1)S(1)} collective-permute-done((bf16[1,1,2,256,1024]{4,3,2,1,0:T(8,128)(2,1)S(1)}, bf16[1,1,2,256,1024]{4,3,2,1,0:T(8,128)(2,1)S(1)}, u32[]{:S(2)}, u32[]{:S(2)}) %collective-permute-start) | collective-permute-done | bytes 1048608 | tf_op jit(solution)/shard_map/ppermute | solution.py:98
  72.2 5.5 collective-permute-start.2
  84.0 6.2 convert_reduce_fusion.1
  93.2 5.5 collective-permute-done.5
  99.8 5.5 collective-permute-start.3
  117.8 3.8 add_convert_fusion.1
  121.7 5.1 collective-permute-done.3
  126.8 4.4 collective-permute-start.4
  137.0 25.2 %shard_map.373 = bf16[4,2,256,256]{3,2,1,0:T(8,128)(2,1)} custom-call(bf16[4,2,256,768]{3,2,1,0:T(8,128)(2,1)S(1)} %bitcast.199, f32[1024,128]{1,0:T(8,128)S(1)} %copy.82.cosine_ref, f32[1024,128]{1,0:T(8,128)S(1)} %copy.83.sine_ref), custom_call_target="tpu_custom_call" | custom-call | flops 4294967296 | bytes 8388608 | tf_op jit(solution)/shard_map/pallas_call | solution.py:269
  167.8 13.3 %all-to-all-done.1 = bf16[4,2,256,256]{3,2,1,0:T(8,128)(2,1)S(1)} async-done(((bf16[4,2,256,256]{3,2,1,0:T(8,128)(2,1)}), bf16[4,2,256,256]{3,2,1,0:T(8,128)(2,1)S(1)}, u32[]{:S(2)}, u32[]{:S(2)}) %all-to-all-start.1) | async-done | bytes 1048608 | tf_op jit(solution)/shard_map/all_to_all | solution.py:479
  187.9 10.1 %all-gather.12.cloned.1.call-done = bf16[1024,684]{0,1:T(8,128)(2,1)} async-done(((bf16[128,684]{0,1:T(8,128)(2,1)}), bf16[1024,684]{0,1:T(8,128)(2,1)}) %all-gather.12.cloned.1.call-update) | async-done | bytes 1400848 | tf_op jit(solution)/shard_map/all_gather | solution.py:453
  209.3 71.5 %all-gather.14.cloned.1.call-done = bf16[8,256,1024]{2,1,0:T(8,128)(2,1)} async-done(((bf16[2,256,1024]{2,1,0:T(8,128)(2,1)}), bf16[8,256,1024]{2,1,0:T(8,128)(2,1)}) %all-gather.14.cloned.1.call-update) | async-done | bytes 4194320 | tf_op jit(solution)/shard_map/all_gather | solution.py:79
  280.8 5.5 fusion.65
  286.3 7.6 %fusion.57 = (bf16[2048]{0:T(1024)(128)(2,1)S(1)}, bf16[2048]{0:T(1024)(128)(2,1)S(1)}, f32[2048,684]{0,1:T(8,128)}, f32[2048,684]{0,1:T(8,128)}) fusion(f32[684]{0:T(1024)S(1)} %fusion.54, f32[684]{0:T(1024)S(1)} %convert_element_type.487, f32[2048,684]{0,1:T(8,128)S(1)} %fusion.65, f32[684]{0:T(1024)S(1)} %convert_element_type.486, ...), kind=kOutput, calls=%fused_computation.192 | convolution fusion | flops 2884308992 | bytes 22421520 | tf_op jit(solution)/shard_map/dot_general | solution.py:303
  294.0 9.5 %psum.42 = bf16[2,2048]{1,0:T(2,128)(2,1)S(1)} all-reduce(bf16[2,2048]{1,0:T(2,128)(2,1)S(1)} %pad_maximum_fusion.3), channel_id=1, replica_groups=mesh['fsdp'=2,'heads'=4,'tensor'=4] {'tensor'}, use_global_device_ids=true, to_apply=%region_6.7 | all-reduce | flops 4096 | bytes 16384 | tf_op jit(solution)/shard_map/psum | solution.py:83
  303.5 3.6 multiply_convert_fusion.2
  308.8 4.1 fusion.66
  315.5 10.7 %multiply_reduce_fusion.1 = (f32[684]{0:T(1024)S(1)}, bf16[2048]{0:T(1024)(128)(2,1)S(1)}, bf16[2048]{0:T(1024)(128)(2,1)S(1)}, f32[684]{0:T(1024)S(1)}, f32[2048,684]{0,1:T(8,128)}) fusion(f32[2048,684]{0,1:T(8,128)} %get-tuple-element.97, f32[2048]{0:T(1024)S(1)} %add_rsqrt_fusion, f32[2048]{0:T(1024)S(1)} %bitcast.243, f32[684]{0:T(1024)S(1)} %fusion.54, ...), kind=kOutput, calls=%fused_computation.11 | convolution fusion | flops 2882906624 | bytes 16837312 | tf_op jit(solution)/shard_map/dot_general | solution.py:73
  326.2 9.9 %psum.43 = bf16[2,2048]{1,0:T(2,128)(2,1)S(1)} all-reduce(bf16[2,2048]{1,0:T(2,128)(2,1)S(1)} %pad_maximum_fusion.4), channel_id=1, replica_groups=mesh['fsdp'=2,'heads'=4,'tensor'=4] {'tensor'}, use_global_device_ids=true, to_apply=%region_9.10 | all-reduce | flops 4096 | bytes 16384 | tf_op jit(solution)/shard_map/psum | solution.py:83
  336.3 12.9 %convert_reduce_fusion.2 = (f32[684]{0:T(1024)S(1)}, bf16[2048,684]{0,1:T(8,128)(2,1)}, f32[684]{0:T(1024)S(1)}, bf16[2048,684]{0,1:T(8,128)(2,1)}) fusion(f32[2048,684]{0,1:T(8,128)} %copy-done.19, f32[684]{0:T(1024)S(1)} %convert_element_type.486, f32[2048]{0:T(1024)S(1)} %bitcast.246, f32[2048]{0:T(1024)S(1)} %add_rsqrt_fusion, ...), kind=kLoop, calls=%fused_computation.12 | loop fusion | flops 40622760 | bytes 28065824 | tf_op jit(solution)/shard_map/reduce_sum | solution.py:338
  349.2 23.9 %reduce-scatter.19.cloned.1.call-done = bf16[128,684]{1,0:T(8,128)(2,1)} async-done(((bf16[1024,684]{1,0:T(8,128)(2,1)}), bf16[128,684]{1,0:T(8,128)(2,1)}) %reduce-scatter.19.cloned.1.call-update) | async-done | bytes 175120
  374.2 5.9 fusion.67
  380.1 5.3 add_convert_fusion
  385.4 7.3 %convolution_convert_fusion.3 = bf16[1024,684]{0,1:T(8,128)(2,1)} fusion(bf16[2048,1024]{1,0:T(8,128)(2,1)} %bitcast.254, bf16[2048,684]{0,1:T(8,128)(2,1)} %get-tuple-element.94), kind=kOutput, calls=%fused_computation.77 | convolution fusion | flops 2869604352 | bytes 8396800 | tf_op jit(solution)/shard_map/dot_general | solution.py:67
  395.7 7.3 %convolution_convert_fusion.4 = bf16[1024,684]{0,1:T(8,128)(2,1)} fusion(bf16[2048,1024]{1,0:T(8,128)(2,1)} %bitcast.255, bf16[2048,684]{0,1:T(8,128)(2,1)} %get-tuple-element.54), kind=kOutput, calls=%fused_computation.78 | convolution fusion | flops 2869604352 | bytes 8396800 | tf_op jit(solution)/shard_map/dot_general | solution.py:67
  405.5 25.4 %all-reduce.9 = (f32[684]{0:T(1024)}, f32[684]{0:T(1024)}, f32[684]{0:T(1024)}, f32[684]{0:T(1024)}) all-reduce(f32[684]{0:T(1024)S(1)} %get-tuple-element.102, f32[684]{0:T(1024)S(1)} %get-tuple-element.93, f32[684]{0:T(1024)S(1)} %get-tuple-element.63, ...), channel_id=1, replica_groups=mesh['fsdp'=2,'heads'=4,'tensor'=4] {'fsdp','heads'}, use_global_device_ids=true, to_apply=%region_13.14 | all-reduce | flops 2736 | bytes 21888 | tf_op jit(solution)/shard_map/psum | solution.py:549
  430.9 31.5 %reduce-scatter.13.cloned.1.call-done = bf16[2,256,1024]{2,1,0:T(8,128)(2,1)} async-done(((bf16[8,256,1024]{2,1,0:T(8,128)(2,1)}), bf16[2,256,1024]{2,1,0:T(8,128)(2,1)}) %reduce-scatter.13.cloned.1.call-update) | async-done | bytes 1048592 | tf_op jit(solution)/shard_map/reduce_scatter | solution.py:164
  474.7 5.8 convolution_convert_fusion
  486.2 4.4 collective-permute-start.14
  496.5 46.3 %shard_map.374 = bf16[4,2,256,768]{3,2,1,0:T(8,128)(2,1)S(1)} custom-call(bf16[4,2,256,768]{3,2,1,0:T(8,128)(2,1)} %bitcast.200, bf16[4,2,256,256]{3,2,1,0:T(8,128)(2,1)S(1)} %copy-done.1, f32[1024,128]{1,0:T(8,128)S(1)} %copy-done.5, f32[1024,128]{1,0:T(8,128)S(1)} %copy-done.3), custom_call_target="tpu_custom_call" | custom-call | flops 10737418240 | bytes 8388608 | tf_op jit(solution)/shard_map/pallas_call | solution.py:269
  553.9 7.7 %fusion.56 = (bf16[1024]{0:T(1024)(128)(2,1)S(1)}, bf16[1024]{0:T(1024)(128)(2,1)S(1)}, bf16[2048,1024]{1,0:T(8,128)(2,1)}) fusion(f32[2048]{0:T(1024)S(1)} %bitcast.249, f32[2048]{0:T(1024)S(1)} %bitcast.248, bf16[2,2,2,256,1024]{4,3,2,1,0:T(8,128)(2,1)} %get-tuple-element.101, bf16[2048,768]{1,0:T(8,128)(2,1)S(1)} %bitcast.198, ...), kind=kOutput, calls=%fused_computation.191 | convolution fusion | flops 3235903488 | bytes 13127680 | tf_op jit(solution)/shard_map/dot_general | solution.py:73
  565.0 4.5 constant_dynamic-slice_fusion
  578.8 5.6 collective-permute-start.16
  585.2 7.2 %collective-permute-done.22 = bf16[576,768]{1,0:T(8,128)(2,1)} collective-permute-done((bf16[576,768]{1,0:T(8,128)(2,1)}, bf16[576,768]{1,0:T(8,128)(2,1)}, u32[]{:S(2)}, u32[]{:S(2)}) %collective-permute-start.22) | collective-permute-done | bytes 884768 | tf_op jit(solution)/shard_map/ppermute | solution.py:117
  594.8 15.9 %collective-permute-done.16 = bf16[2,256,1024]{2,1,0:T(8,128)(2,1)} collective-permute-done((bf16[2,256,1024]{2,1,0:T(8,128)(2,1)}, bf16[2,256,1024]{2,1,0:T(8,128)(2,1)}, u32[]{:S(2)}, u32[]{:S(2)}) %collective-permute-start.16) | collective-permute-done | bytes 1048608 | tf_op jit(solution)/shard_map/ppermute | solution.py:159
  610.7 4.1 fusion.17
  621.3 6.1 collective-permute-start.17
  635.5 6.5 reduce-scatter.15.cloned.1.call-done
  643.7 3.7 all-to-all-start.3
  647.4 4.8 collective-permute-done.18
  656.3 5.8 all-to-all-done.3
  671.2 3.9 fusion.11
  675.1 6.9 collective-permute-done.19
  682.1 3.6 fusion.22
  (362 shorter events, 163.6 us)
Async XLA Ops:
  7.2 39.3 %copy-start.11 = (bf16[2,256,1024]{2,1,0:T(8,128)(2,1)S(1)}, bf16[2,256,1024]{2,1,0:T(8,128)(2,1)}, u32[]{:S(2)}) copy-start(bf16[2,256,1024]{2,1,0:T(8,128)(2,1)} %param.22) | copy-start | bytes 3145732
  7.2 74.1 %all-gather.18.cloned.1.call-start = ((), (), s32[]{:S(2)}) async-start(), calls=%async_computation.18 | async-start | bytes 1880064 | tf_op jit(solution)/shard_map/all_gather | solution.py:419
  22.5 159.7 %all-gather.8.cloned.1.call-start = ((), (), s32[]{:S(2)}) async-start(), calls=%async_computation.10 | async-start | bytes 2359296 | tf_op jit(solution)/shard_map/all_gather | solution.py:442
  22.6 5.4 collective-permute-start.8
  26.1 6.2 collective-permute-start.11
  27.9 6.8 collective-permute-start.9
  32.2 7.1 %collective-permute-start.12 = (bf16[32,1024]{1,0:T(8,128)(2,1)S(1)}, bf16[32,1024]{1,0:T(8,128)(2,1)S(1)}, u32[]{:S(2)}, u32[]{:S(2)}) collective-permute-start(bf16[32,1024]{1,0:T(8,128)(2,1)S(1)} %collective-permute-done.11), channel_id=1, source_target_pairs={{1,0},{2,1},{3,2},{5,4},{6,5},{7,6},{9,8},{10,9},{11,10},{13,12},{... | collective-permute-start | bytes 196616 | tf_op jit(solution)/shard_map/ppermute | solution.py:130
  34.8 7.0 %collective-permute-start.10 = (bf16[32,1024]{1,0:T(8,128)(2,1)S(1)}, bf16[32,1024]{1,0:T(8,128)(2,1)S(1)}, u32[]{:S(2)}, u32[]{:S(2)}) collective-permute-start(bf16[32,1024]{1,0:T(8,128)(2,1)S(1)} %collective-permute-done.9), channel_id=1, source_target_pairs={{0,1},{1,2},{2,3},{4,5},{5,6},{6,7},{8,9},{9,10},{10,11},{12,13},{... | collective-permute-start | bytes 196616 | tf_op jit(solution)/shard_map/ppermute | solution.py:129
  39.3 6.4 collective-permute-start.13
  41.8 28.6 %copy-start.56 = (s32[2]{0:T(128)S(1)}, s32[2]{0:T(128)}, u32[]{:S(2)}) copy-start(s32[2]{0:T(128)} %param.23) | copy-start | bytes 28
  46.4 141.5 %all-gather.10.cloned.1.call-start = ((), (), s32[]{:S(2)}) async-start(), calls=%async_computation.11 | async-start | bytes 1585152 | tf_op jit(solution)/shard_map/all_gather | solution.py:452
  46.5 22.2 %collective-permute-start = (bf16[1,1,2,256,1024]{4,3,2,1,0:T(8,128)(2,1)S(1)}, bf16[1,1,2,256,1024]{4,3,2,1,0:T(8,128)(2,1)S(1)}, u32[]{:S(2)}, u32[]{:S(2)}) collective-permute-start(bf16[1,1,2,256,1024]{4,3,2,1,0:T(8,128)(2,1)S(1)} %bitcast.201), channel_id=1, source_target_pairs={{0,8},{4,12},{8,0},{12,4},{1,9},{5,13},{9,1},{13,5},{2,10},{6,14},... | collective-permute-start | bytes 3145736 | tf_op jit(solution)/shard_map/ppermute | solution.py:98
  70.4 13.6 %collective-permute-start.1 = (bf16[2,1,2,256,1024]{4,3,2,1,0:T(8,128)(2,1)}, bf16[2,1,2,256,1024]{4,3,2,1,0:T(8,128)(2,1)}, u32[]{:S(2)}, u32[]{:S(2)}) collective-permute-start(bf16[2,1,2,256,1024]{4,3,2,1,0:T(8,128)(2,1)} %maximum_select_fusion.1), channel_id=1, source_target_pairs={{0,4},{4,0},{8,12},{12,8},{1,5},{5,1},{9,13},{13,9},{2,6},{6,2},{1... | collective-permute-start | bytes 6291464 | tf_op jit(solution)/shard_map/ppermute | solution.py:98
  70.4 394.5 %copy-start.45 = (f32[2]{0:T(128)}, f32[2]{0:T(128)S(1)}, u32[]{:S(2)}) copy-start(f32[2]{0:T(128)S(1)} %convert_element_type.460) | copy-start | bytes 28
  70.9 27.8 %collective-permute-start.5 = (bf16[2,256,1024]{2,1,0:T(8,128)(2,1)S(1)}, bf16[2,256,1024]{2,1,0:T(8,128)(2,1)}, u32[]{:S(2)}, u32[]{:S(2)}) collective-permute-start(bf16[2,256,1024]{2,1,0:T(8,128)(2,1)S(1)} %get-tuple-element.90), channel_id=1, source_target_pairs={{1,0},{2,1},{3,2},{5,4},{6,5},{7,6},{9,8},{10,9},{11,10},{13,12},{... | collective-permute-start | bytes 3145736 | tf_op jit(solution)/shard_map/ppermute | solution.py:130
  72.2 27.6 %collective-permute-start.2 = (bf16[2,256,1024]{2,1,0:T(8,128)(2,1)S(1)}, bf16[2,256,1024]{2,1,0:T(8,128)(2,1)}, u32[]{:S(2)}, u32[]{:S(2)}) collective-permute-start(bf16[2,256,1024]{2,1,0:T(8,128)(2,1)S(1)} %get-tuple-element.90), channel_id=1, source_target_pairs={{0,1},{1,2},{2,3},{4,5},{5,6},{6,7},{8,9},{9,10},{10,11},{12,13},{... | collective-permute-start | bytes 3145736 | tf_op jit(solution)/shard_map/ppermute | solution.py:129
  78.9 58.1 %copy-start.2 = (f32[1024,128]{1,0:T(8,128)}, f32[1024,128]{1,0:T(8,128)S(1)}, u32[]{:S(2)}) copy-start(f32[1024,128]{1,0:T(8,128)S(1)} %copy.83.sine_ref) | copy-start | bytes 1572868
  81.3 55.7 %copy-start.4 = (f32[1024,128]{1,0:T(8,128)}, f32[1024,128]{1,0:T(8,128)S(1)}, u32[]{:S(2)}) copy-start(f32[1024,128]{1,0:T(8,128)S(1)} %copy.82.cosine_ref) | copy-start | bytes 1572868
  99.8 27.0 %collective-permute-start.3 = (bf16[2,256,1024]{2,1,0:T(8,128)(2,1)}, bf16[2,256,1024]{2,1,0:T(8,128)(2,1)}, u32[]{:S(2)}, u32[]{:S(2)}) collective-permute-start(bf16[2,256,1024]{2,1,0:T(8,128)(2,1)} %collective-permute-done.2), channel_id=1, source_target_pairs={{0,1},{1,2},{2,3},{4,5},{5,6},{6,7},{8,9},{9,10},{10,11},{12,13},{... | collective-permute-start | bytes 3145736 | tf_op jit(solution)/shard_map/ppermute | solution.py:129
  105.3 26.6 %collective-permute-start.6 = (bf16[2,256,1024]{2,1,0:T(8,128)(2,1)}, bf16[2,256,1024]{2,1,0:T(8,128)(2,1)}, u32[]{:S(2)}, u32[]{:S(2)}) collective-permute-start(bf16[2,256,1024]{2,1,0:T(8,128)(2,1)} %collective-permute-done.5), channel_id=1, source_target_pairs={{1,0},{2,1},{3,2},{5,4},{6,5},{7,6},{9,8},{10,9},{11,10},{13,12},{... | collective-permute-start | bytes 3145736 | tf_op jit(solution)/shard_map/ppermute | solution.py:130
  126.8 35.5 %collective-permute-start.4 = (bf16[2,256,1024]{2,1,0:T(8,128)(2,1)}, bf16[2,256,1024]{2,1,0:T(8,128)(2,1)S(1)}, u32[]{:S(2)}, u32[]{:S(2)}) collective-permute-start(bf16[2,256,1024]{2,1,0:T(8,128)(2,1)} %collective-permute-done.3), channel_id=1, source_target_pairs={{0,1},{1,2},{2,3},{4,5},{5,6},{6,7},{8,9},{9,10},{10,11},{12,13},{... | collective-permute-start | bytes 3145736 | tf_op jit(solution)/shard_map/ppermute | solution.py:129
  131.8 31.4 %collective-permute-start.7 = (bf16[2,256,1024]{2,1,0:T(8,128)(2,1)}, bf16[2,256,1024]{2,1,0:T(8,128)(2,1)}, u32[]{:S(2)}, u32[]{:S(2)}) collective-permute-start(bf16[2,256,1024]{2,1,0:T(8,128)(2,1)} %collective-permute-done.6), channel_id=1, source_target_pairs={{1,0},{2,1},{3,2},{5,4},{6,5},{7,6},{9,8},{10,9},{11,10},{13,12},{... | collective-permute-start | bytes 3145736 | tf_op jit(solution)/shard_map/ppermute | solution.py:130
  163.2 17.9 %all-to-all-start.1 = ((bf16[4,2,256,256]{3,2,1,0:T(8,128)(2,1)}), bf16[4,2,256,256]{3,2,1,0:T(8,128)(2,1)S(1)}, u32[]{:S(2)}, u32[]{:S(2)}) async-start(bf16[4,2,256,256]{3,2,1,0:T(8,128)(2,1)} %shard_map.373), calls=%async_computation.1 | async-start | bytes 2097152 | tf_op jit(solution)/shard_map/all_to_all | solution.py:479
  166.7 31.3 %all-gather.12.cloned.1.call-start = ((), (), s32[]{:S(2)}) async-start(), calls=%async_computation.12 | async-start | bytes 1585152 | tf_op jit(solution)/shard_map/all_gather | solution.py:453
  167.3 113.5 %all-gather.14.cloned.1.call-start = ((), (), s32[]{:S(2)}) async-start(), calls=%async_computation.13 | async-start | bytes 5242880 | tf_op jit(solution)/shard_map/all_gather | solution.py:79
  186.1 278.9 %copy-start.7 = (f32[2,256,1024]{2,1,0:T(8,128)}, f32[2,256,1024]{2,1,0:T(8,128)S(1)}, u32[]{:S(2)}) copy-start(f32[2,256,1024]{2,1,0:T(8,128)S(1)} %get-tuple-element.99) | copy-start | bytes 6291460
  198.0 117.4 %all-gather.16.cloned.1.call-start = ((), (), s32[]{:S(2)}) async-start(), calls=%async_computation.14 | async-start | bytes 1585152 | tf_op jit(solution)/shard_map/all_gather | solution.py:454
  198.6 174.4 %reduce-scatter.19.cloned.1.call-start = ((), (), s32[]{:S(2)}) async-start(), calls=%async_computation.19 | async-start | bytes 1769472
  336.2 126.1 %reduce-scatter.13.cloned.1.call-start = ((), (), s32[]{:S(2)}) async-start(), calls=%async_computation.15 | async-start | bytes 5242880 | tf_op jit(solution)/shard_map/reduce_scatter | solution.py:164
  385.4 232.2 %reduce-scatter.23.cloned.1.call-start = ((), (), s32[]{:S(2)}) async-start(), calls=%async_computation.21 | async-start | bytes 1769472
  395.3 224.1 %reduce-scatter.21.cloned.1.call-start = ((), (), s32[]{:S(2)}) async-start(), calls=%async_computation.20 | async-start | bytes 1769472
  471.1 21.0 %all-to-all-start.2 = ((bf16[4,2,256,256]{3,2,1,0:T(8,128)(2,1)}), bf16[4,2,256,256]{3,2,1,0:T(8,128)(2,1)S(1)}, u32[]{:S(2)}, u32[]{:S(2)}) async-start(bf16[4,2,256,256]{3,2,1,0:T(8,128)(2,1)} %bitcast.195), calls=%async_computation.3 | async-start | bytes 2097152 | tf_op jit(solution)/shard_map/all_to_all | solution.py:561
  474.6 152.7 %reduce-scatter.17.cloned.1.call-start = ((), (), s32[]{:S(2)}) async-start(), calls=%async_computation.17 | async-start | bytes 327680 | tf_op jit(solution)/shard_map/reduce_scatter | solution.py:648
  483.0 59.8 %collective-permute-start.23 = (bf16[512,1024]{1,0:T(8,128)(2,1)}, bf16[512,1024]{1,0:T(8,128)(2,1)}, u32[]{:S(2)}, u32[]{:S(2)}) collective-permute-start(bf16[512,1024]{1,0:T(8,128)(2,1)} %dynamic-slice_bitcast_fusion.1), channel_id=1, source_target_pairs={{0,16},{16,0},{1,17},{17,1},{2,18},{18,2},{3,19},{19,3},{4,20},{20... | collective-permute-start | bytes 3145736 | tf_op jit(solution)/shard_map/ppermute | solution.py:117
  486.2 60.1 %collective-permute-start.14 = (bf16[2,256,1024]{2,1,0:T(8,128)(2,1)}, bf16[2,256,1024]{2,1,0:T(8,128)(2,1)}, u32[]{:S(2)}, u32[]{:S(2)}) collective-permute-start(bf16[2,256,1024]{2,1,0:T(8,128)(2,1)} %get-tuple-element.56), channel_id=1, source_target_pairs={{0,1},{1,2},{2,3},{4,5},{5,6},{6,7},{8,9},{9,10},{10,11},{12,13},{... | collective-permute-start | bytes 3145736 | tf_op jit(solution)/shard_map/ppermute | solution.py:159
  490.6 55.6 %collective-permute-start.15 = (bf16[2,256,1024]{2,1,0:T(8,128)(2,1)}, bf16[2,256,1024]{2,1,0:T(8,128)(2,1)}, u32[]{:S(2)}, u32[]{:S(2)}) collective-permute-start(bf16[2,256,1024]{2,1,0:T(8,128)(2,1)} %get-tuple-element.57), channel_id=1, source_target_pairs={{1,0},{2,1},{3,2},{5,4},{6,5},{7,6},{9,8},{10,9},{11,10},{13,12},{... | collective-permute-start | bytes 3145736 | tf_op jit(solution)/shard_map/ppermute | solution.py:159
  496.5 46.3 %copy-start.31 = (bf16[1024,1024]{1,0:T(8,128)(2,1)S(1)}, bf16[1024,1024]{1,0:T(8,128)(2,1)}, u32[]{:S(2)}) copy-start(bf16[1024,1024]{1,0:T(8,128)(2,1)} %copy-done.30) | copy-start | bytes 6291460
  546.3 26.4 %collective-permute-start.24 = (bf16[2,128,1024]{2,1,0:T(8,128)(2,1)}, bf16[2,128,1024]{2,1,0:T(8,128)(2,1)}, u32[]{:S(2)}, u32[]{:S(2)}) collective-permute-start(bf16[2,128,1024]{2,1,0:T(8,128)(2,1)} %dynamic-slice_bitcast_fusion.4), channel_id=1, source_target_pairs={{0,4},{4,0},{8,12},{12,8},{1,5},{5,1},{9,13},{13,9},{2,6},{6,2},{1... | collective-permute-start | bytes 1572872 | tf_op jit(solution)/shard_map/ppermute | solution.py:117
  570.5 22.0 %collective-permute-start.22 = (bf16[576,768]{1,0:T(8,128)(2,1)}, bf16[576,768]{1,0:T(8,128)(2,1)}, u32[]{:S(2)}, u32[]{:S(2)}) collective-permute-start(bf16[576,768]{1,0:T(8,128)(2,1)} %bitcast.196), channel_id=1, source_target_pairs={{0,16},{16,0},{1,17},{17,1},{2,18},{18,2},{3,19},{19,3},{4,20},{20... | collective-permute-start | bytes 2654216 | tf_op jit(solution)/shard_map/ppermute | solution.py:117
  572.6 56.2 %collective-permute-start.20 = (bf16[2,2,256,1024]{3,2,1,0:T(8,128)(2,1)}, bf16[2,2,256,1024]{3,2,1,0:T(8,128)(2,1)}, u32[]{:S(2)}, u32[]{:S(2)}) collective-permute-start(bf16[2,2,256,1024]{3,2,1,0:T(8,128)(2,1)} %dynamic-slice_bitcast_fusion), channel_id=1, source_target_pairs={{0,4},{4,0},{8,12},{12,8},{1,5},{5,1},{9,13},{13,9},{2,6},{6,2},{1... | collective-permute-start | bytes 6291464 | tf_op jit(solution)/shard_map/ppermute | solution.py:117
  573.9 10.5 %collective-permute-start.25 = (bf16[128,1024]{1,0:T(8,128)(2,1)S(1)}, bf16[128,1024]{1,0:T(8,128)(2,1)S(1)}, u32[]{:S(2)}, u32[]{:S(2)}) collective-permute-start(bf16[128,1024]{1,0:T(8,128)(2,1)S(1)} %fusion.30), channel_id=1, source_target_pairs={{0,8},{4,12},{8,0},{12,4},{1,9},{5,13},{9,1},{13,5},{2,10},{6,14},... | collective-permute-start | bytes 786440 | tf_op jit(solution)/shard_map/ppermute | solution.py:117
  578.8 31.9 %collective-permute-start.16 = (bf16[2,256,1024]{2,1,0:T(8,128)(2,1)}, bf16[2,256,1024]{2,1,0:T(8,128)(2,1)}, u32[]{:S(2)}, u32[]{:S(2)}) collective-permute-start(bf16[2,256,1024]{2,1,0:T(8,128)(2,1)} %fusion.16), channel_id=1, source_target_pairs={{0,1},{1,2},{2,3},{4,5},{5,6},{6,7},{8,9},{9,10},{10,11},{12,13},{... | collective-permute-start | bytes 3145736 | tf_op jit(solution)/shard_map/ppermute | solution.py:159
  585.2 56.8 %reduce-scatter.15.cloned.1.call-start = ((), (), s32[]{:S(2)}) async-start(), calls=%async_computation.16 | async-start | bytes 1105920 | tf_op jit(solution)/shard_map/reduce_scatter | solution.py:631
  614.8 37.4 %collective-permute-start.18 = (bf16[2,256,1024]{2,1,0:T(8,128)(2,1)S(1)}, bf16[2,256,1024]{2,1,0:T(8,128)(2,1)S(1)}, u32[]{:S(2)}, u32[]{:S(2)}) collective-permute-start(bf16[2,256,1024]{2,1,0:T(8,128)(2,1)S(1)} %get-tuple-element.61), channel_id=1, source_target_pairs={{1,0},{2,1},{3,2},{5,4},{6,5},{7,6},{9,8},{10,9},{11,10},{13,12},{... | collective-permute-start | bytes 3145736 | tf_op jit(solution)/shard_map/ppermute | solution.py:159
  621.3 53.9 %collective-permute-start.17 = (bf16[2,256,1024]{2,1,0:T(8,128)(2,1)}, bf16[2,256,1024]{2,1,0:T(8,128)(2,1)}, u32[]{:S(2)}, u32[]{:S(2)}) collective-permute-start(bf16[2,256,1024]{2,1,0:T(8,128)(2,1)} %get-tuple-element.60), channel_id=1, source_target_pairs={{0,1},{1,2},{2,3},{4,5},{5,6},{6,7},{8,9},{9,10},{10,11},{12,13},{... | collective-permute-start | bytes 3145736 | tf_op jit(solution)/shard_map/ppermute | solution.py:159
  635.1 33.1 %collective-permute-start.21 = (bf16[2,256,1024]{2,1,0:T(8,128)(2,1)}, bf16[2,256,1024]{2,1,0:T(8,128)(2,1)}, u32[]{:S(2)}, u32[]{:S(2)}) collective-permute-start(bf16[2,256,1024]{2,1,0:T(8,128)(2,1)} %fusion.27), channel_id=1, source_target_pairs={{0,8},{4,12},{8,0},{12,4},{1,9},{5,13},{9,1},{13,5},{2,10},{6,14},... | collective-permute-start | bytes 3145736 | tf_op jit(solution)/shard_map/ppermute | solution.py:117
  643.7 18.4 %all-to-all-start.3 = ((bf16[4,36,768]{2,1,0:T(8,128)(2,1)}), bf16[4,36,768]{2,1,0:T(8,128)(2,1)S(1)}, u32[]{:S(2)}, u32[]{:S(2)}) async-start(bf16[4,36,768]{2,1,0:T(8,128)(2,1)} %all_to_all.18), calls=%async_computation.5 | async-start | bytes 491520 | tf_op jit(solution)/shard_map/all_to_all | solution.py:632
  654.8 27.2 %collective-permute-start.19 = (bf16[2,256,1024]{2,1,0:T(8,128)(2,1)}, bf16[2,256,1024]{2,1,0:T(8,128)(2,1)}, u32[]{:S(2)}, u32[]{:S(2)}) collective-permute-start(bf16[2,256,1024]{2,1,0:T(8,128)(2,1)} %fusion.15), channel_id=1, source_target_pairs={{1,0},{2,1},{3,2},{5,4},{6,5},{7,6},{9,8},{10,9},{11,10},{13,12},{... | collective-permute-start | bytes 3145736 | tf_op jit(solution)/shard_map/ppermute | solution.py:159
  (50 other events, 421.2 us)
Sparse Core Ops, SparseCore 0:
  22.6 46.1 all-gather.17
  71.3 26.1 all-gather.7
  99.4 25.0 all-gather.9
  169.1 28.8 all-gather.11
  200.0 80.7 all-gather.13
  282.5 23.5 all-gather.15
  336.3 36.6 reduce-scatter.18
  385.5 76.7 reduce-scatter.12
  465.6 45.3 reduce-scatter.22
  514.1 38.4 reduce-scatter.20
  585.3 21.7 reduce-scatter.16
  609.2 32.6 reduce-scatter.14
